TPU v7x, 512 devices: a whole 4x8x8 slice. The times are simulated.
512 devices in a mesh: dp: 8 (over y), slab: 16 (over x_hi, z), view: 4 (over x_lo, core).
Axes of the slice: x: 4 (x_hi: 2, x_lo: 2; x = x_hi * 2 + x_lo), y: 8, z: 8, core: 2. Of those that a mesh axis runs over, the one named last changes fastest.
Arguments:
- latent_feats: bfloat16 [8, 4, 64, 32, 256], P('dp', 'view', 'slab'), may hold values from -6 to 6
- conv_weight: bfloat16 [2304, 256], P(('dp', 'slab')), may hold values from -0.125 to 0.125
- kv_weight: bfloat16 [256, 1536], P(('dp', 'slab')), may hold values from -0.375 to 0.375
- stream: bfloat16 [8, 4, 64, 32, 768], P('dp', 'view', 'slab'), may hold values from -6 to 6
- queries: bfloat16 [8, 4, 64, 32, 768], P('dp', 'view', 'slab'), may hold values from -102 to 102
- norm_gain: float32 [768], replicated, may hold values from 0.1 to 1.9
- up_weight: bfloat16 [768, 3072], P(('dp', 'slab'), 'view'), may hold values from -0.21875 to 0.21875
- down_weight: bfloat16 [768, 3072], P(('dp', 'slab'), 'view'), may hold values from -0.109375 to 0.109375
- band_start: int32 [8, 4, 64, 4], P('dp', 'view', 'slab'), may hold values from 0 to 63, as said below
- band_end: int32 [8, 4, 64, 4], P('dp', 'view', 'slab'), may hold values from 1 to 64
- visibility: int32 [8, 4, 4], P('dp'), may hold values 0 or 1
Outputs:
- output: bfloat16 [8, 4, 64, 32, 768], P('dp', 'view', 'slab')
Inputs may be any that keep to these rules, and one draw needn't show every extreme that they name: band_end - band_start lies in 1 to 4 and equals 4 for some rows in every draw; for a row r both bounds lie within rows (r // 4) * 4 - 1 to (r // 4 + 1) * 4 + 1, clipped to the grid.
All inputs are finite; a program needn't handle non-finite values. No bound on the sum of `visibility` on one device may be relied on, other than what follows from the above.
Results may differ from a plain program's by a relative error of at most 0.0085.
Values may be sent and summed in bfloat16 or wider, within the bound.
No kernel may reach another device: no remote copies, remote signals or barrier semaphores. Data moves between devices by JAX's collectives and lax.ppermute only.
A program may use at most 64 MiB of HBM per device.

v0:
```python
import jax
import jax.numpy as jnp
import numpy as np
from jax import lax
from jax.experimental import pallas as pl
from jax.experimental.pallas import tpu as pltpu
from jax.sharding import Mesh
from jax.sharding import PartitionSpec as P

HEAD_DIM = 64
SLAB = ("slab_0", "slab_1")
DP_SLAB = ("dp", "slab_0", "slab_1")
BF = jnp.bfloat16
F32 = jnp.float32

VMEM = pl.BlockSpec(memory_space=pltpu.VMEM)
HBM = pl.BlockSpec(memory_space=pltpu.HBM)
SMEM = pl.BlockSpec(memory_space=pltpu.SMEM)


def one_hot(size, rows):
    place = lax.broadcasted_iota(jnp.int32, (1, size), 1)
    z = place // (16 * rows)
    rest = place % (16 * rows)
    row = (rest // rows * 8 + z) * rows + rest % rows
    here = lax.broadcasted_iota(jnp.int32, (size, size), 0)
    return jnp.where(here == row, 1.0, 0.0).astype(BF)


def conv_kernel(where_ref, rows_ref, own_ref, other_ref, out_ref, x_ref, weight_ref, sem):
    copy = pltpu.make_async_copy(rows_ref, x_ref, sem)
    copy.start()
    for core, ref in ((0, own_ref), (1, other_ref)):

        @pl.when(where_ref[0] == core)
        def _(ref=ref):
            for tile in range(2):
                cols = slice(tile * 128, (tile + 1) * 128)
                for d in range(8):
                    rows = slice(d * 288, (d + 1) * 288)
                    weight_ref[rows, cols] = ref[d, tile * 288 : (tile + 1) * 288, :]

    copy.wait()
    x = x_ref[...].astype(F32)
    col = lax.broadcasted_iota(jnp.int32, x.shape, 0) % 32
    left = jnp.where(col == 0, 0.0, pltpu.roll(x, 1, 0)).astype(BF)
    right = jnp.where(col == 31, 0.0, pltpu.roll(x, x.shape[0] - 1, 0)).astype(BF)
    shifted = (left, x_ref[...], right)
    conv = jnp.zeros((192, 256), F32)
    for tap in range(9):
        rows = shifted[tap % 3][tap // 3 * 32 : tap // 3 * 32 + 192]
        conv = conv + jnp.dot(
            rows, weight_ref[tap * 256 : (tap + 1) * 256, :], preferred_element_type=F32
        )
    silu = conv / (1.0 + jnp.exp(-conv))
    encoded = (x[32:224] + silu).astype(BF)
    out_ref[...] = jnp.dot(encoded, one_hot(256, 2), preferred_element_type=F32).astype(BF)


def attention_kernel(
    where_ref,
    start_ref,
    end_ref,
    seen_ref,
    enc_ref,
    own_ref,
    other_ref,
    q_ref,
    stream_ref,
    gain_ref,
    normed_ref,
    far_ref,
    kv_ref,
    bias_ref,
    residual_ref,
    sems,
):
    first = where_ref[0] == 0
    first_row = where_ref[1]
    enc = enc_ref[...]
    for tile in range(12):
        at = slice(tile * 32, (tile + 1) * 32)
        weight = jnp.concatenate(
            [jnp.where(first, other_ref[z, at, :], own_ref[z, at, :]) for z in range(8)], axis=0
        )
        kv_ref[tile] = jnp.dot(enc, weight, preferred_element_type=F32).astype(BF)
    lane = lax.broadcasted_iota(jnp.int32, (1, 768), 1)
    key_view = lane // 192
    key_row = first_row - 1 + (lane % 192) // 32
    for r in range(4):
        low = jnp.zeros((1, 768), jnp.int32)
        high = jnp.zeros((1, 768), jnp.int32)
        for u in range(4):
            mine = key_view == u
            low = jnp.where(mine, start_ref[r, u], low)
            high = jnp.where(mine, jnp.where(seen_ref[u] == 1, end_ref[r, u], -1), high)
        bias = jnp.where((low <= key_row) & (key_row < high), 0.0, -1e30)
        bias_ref[r * 32 : (r + 1) * 32, :] = jnp.broadcast_to(bias, (32, 768))
    left = lax.broadcasted_iota(jnp.int32, (128, 128), 1) < HEAD_DIM
    square = jnp.zeros((128, 1), F32)
    copies = []
    for pair in range(6):
        q = q_ref[:, pair * 128 : (pair + 1) * 128]
        zero = jnp.zeros_like(q)
        keys = kv_ref[pair]
        values = kv_ref[6 + pair]
        both = jnp.concatenate([jnp.where(left, q, zero), jnp.where(left, zero, q)], axis=0)
        scores = lax.dot_general(
            both, keys, (((1,), (1,)), ((), ())), preferred_element_type=F32
        )
        bias = bias_ref[...]
        scores = scores * HEAD_DIM ** (-0.5) + jnp.concatenate([bias, bias], axis=0)
        weights = jnp.exp(scores - jnp.max(scores, axis=-1, keepdims=True))
        share = 1.0 / jnp.sum(weights, axis=-1, keepdims=True)
        outs = jnp.dot(weights.astype(BF), values, preferred_element_type=F32) * share
        attended = jnp.where(left, outs[:128], outs[128:])
        cols = slice(pair * 128, (pair + 1) * 128)
        residual = stream_ref[:, cols].astype(F32) + attended
        residual_ref[:, cols] = residual
        copies.append(
            pltpu.make_async_copy(residual_ref.at[:, cols], far_ref.at[:, cols], sems.at[pair])
        )
        copies[-1].start()
        square = square + jnp.sum(residual * residual, axis=-1, keepdims=True)
    scale = lax.rsqrt(square * (1.0 / 768) + 1e-6)
    normed_ref[...] = (residual_ref[...] * scale * gain_ref[...]).astype(BF)
    for copy in copies:
        copy.wait()


def gelu(v):
    return 0.5 * v * (1.0 + jnp.tanh(0.7978845608028654 * (v + 0.044715 * (v * v * v))))


def mlp_kernel(tok_ref, w_ref, out_ref, up_ref, down_ref):
    for tile in range(6):
        cols = slice(tile * 128, (tile + 1) * 128)
        for d in range(8):
            rows = slice(d * 96, (d + 1) * 96)
            up_ref[rows, cols] = w_ref[d, tile * 96 : (tile + 1) * 96, :]
            down_ref[rows, cols] = w_ref[d, 576 + tile * 96 : 576 + (tile + 1) * 96, :]

    for block in range(4):
        tokens = tok_ref[block * 128 : (block + 1) * 128, :]
        hidden = gelu(jnp.dot(tokens, up_ref[...], preferred_element_type=F32)).astype(BF)
        out_ref[block] = last_dims(hidden, down_ref[...]).astype(BF)


def swap_kernel(where_ref, tok_ref, out_ref):
    @pl.when(where_ref[0] == 0)
    def _():
        out_ref[...] = tok_ref[...]

    @pl.when(where_ref[0] != 0)
    def _():
        out_ref[...] = jnp.dot(tok_ref[...], one_hot(768, 6), preferred_element_type=F32).astype(BF)


def sum_kernel(parts_ref, residual_ref, out_ref):
    swap = one_hot(768, 6)
    odd = parts_ref[1].astype(F32) + parts_ref[3].astype(F32)
    high = odd.astype(BF)
    low = (odd - high.astype(F32)).astype(BF)
    odd = last_dims(high, swap) + last_dims(low, swap)
    even = parts_ref[0].astype(F32) + parts_ref[2].astype(F32)
    out_ref[...] = (residual_ref[...] + (even + odd)).astype(BF)


def last_dims(a, b):
    return lax.dot_general(a, b, (((1,), (1,)), ((), ())), preferred_element_type=F32)


def pack_kernel(where_ref, *refs):
    (sources, out_ref, held, sems) = (refs[:4], refs[4], refs[5:9], refs[9])
    copies = [pltpu.make_async_copy(sources[k], held[k], sems.at[k]) for k in range(4)]
    for copy in copies:
        copy.start()
    for copy in copies:
        copy.wait()
    conv_ref, kv_ref, up_ref, down_ref = held

    def tiles(ref, count):
        return [ref[:, t * 128 : (t + 1) * 128].astype(F32) for t in range(count)]

    mlp = tiles(up_ref, 6) + tiles(down_ref, 6)

    def put(code):
        block = jnp.concatenate(code + mlp, axis=0).astype(BF)
        for k in range(16):
            out_ref[k] = block

    @pl.when(where_ref[0] == 0)
    def _():
        put(tiles(conv_ref, 2))

    @pl.when(where_ref[0] != 0)
    def _():
        put(tiles(kv_ref, 12) + [jnp.zeros((12, 128), F32)])


def kernel_call(body, out_shape, in_specs, scratch=(), out_specs=None):
    outs = out_specs or jax.tree.map(lambda _: VMEM, out_shape)
    return pl.pallas_call(
        body,
        out_shape=out_shape,
        in_specs=in_specs,
        out_specs=outs,
        scratch_shapes=scratch,
        compiler_params=pltpu.CompilerParams(vmem_limit_bytes=16 << 20),
    )


def in_hbm(value):
    return pltpu.with_memory_space_constraint(value, pltpu.HBM)


def by_core(even, odd):
    ids = np.arange(512).reshape(8, 2, 8, 4)
    groups = []
    for axes, views in ((even, (0, 2)), (odd, (1, 3))):
        held = [axis for axis in range(3) if axis not in axes]
        for view in views:
            lines = ids[..., view].transpose(*held, *axes)
            groups.extend(lines.reshape(-1, int(np.prod([ids.shape[a] for a in axes]))).tolist())
    return groups


def copies_of(value, count):
    return jnp.broadcast_to(value, (count, *value.shape))


def exchange(copies, groups):
    return lax.all_to_all(
        copies,
        ("dp", "slab_0", "slab_1", "view"),
        split_axis=0,
        concat_axis=0,
        axis_index_groups=groups,
        tiled=True,
    )


def regroup(tiles, rows):
    devices = tiles.shape[0]
    tiles = tiles.reshape(devices, -1, rows, 128).swapaxes(0, 1)
    return tiles.reshape(-1, 128)


def shards(
    latent_feats,
    conv_weight,
    kv_weight,
    stream,
    queries,
    norm_gain,
    up_weight,
    down_weight,
    band_start,
    band_end,
    visibility,
):
    view_id = lax.axis_index("view")
    core = view_id % 2
    first_row = lax.axis_index(SLAB) * 4
    where = jnp.stack([core, first_row]).astype(jnp.int32)
    feats = latent_feats[0, 0]
    ends = lax.axis_size(SLAB) - 1
    above = lax.ppermute(feats[2:], SLAB, [(i, i + 1) for i in range(ends)])
    below = lax.ppermute(feats[:2], SLAB, [(i + 1, i) for i in range(ends)])
    rows = jnp.concatenate([above, feats, below], axis=0).reshape(256, 256)

    even = core == 0
    mine = kernel_call(
        pack_kernel,
        jax.ShapeDtypeStruct((16, 108, 128), BF),
        [SMEM] + [HBM] * 4,
        scratch=[pltpu.VMEM(w.shape, BF) for w in (conv_weight, kv_weight, up_weight, down_weight)]
        + [pltpu.SemaphoreType.DMA((4,))],
    )(where, *map(in_hbm, (conv_weight, kv_weight, up_weight, down_weight)))
    wide = by_core((1, 2), (0, 1))
    long = by_core((0,), (2,))
    near = exchange(mine, wide)
    near, rows = lax.optimization_barrier((near, rows))
    code = jnp.where(
        even, regroup(near[:, :36], 18), jnp.pad(regroup(near[:, :24], 2), ((0, 192), (0, 0)))
    )
    units = jnp.concatenate([regroup(near[:, 36:72], 6), regroup(near[:, 72:], 6)], axis=0)
    code = copies_of(code, 8)
    own = exchange(code, long)
    units = copies_of(units, 8)
    other = lax.ppermute(own, "view", [(i, i ^ 1) for i in range(4)])
    mlp = exchange(units, long)

    encoded = kernel_call(
        conv_kernel,
        jax.ShapeDtypeStruct((192, 256), BF),
        [SMEM, HBM, VMEM, VMEM],
        scratch=[
            pltpu.VMEM((256, 256), BF),
            pltpu.VMEM((2304, 256), BF),
            pltpu.SemaphoreType.DMA(()),
        ],
    )(where, in_hbm(rows), own, other)
    nearby = lax.all_gather(encoded, "view", axis=0, tiled=True)
    vis_row = lax.dynamic_index_in_dim(visibility[0], view_id, 0, False)
    seen = jnp.where(jnp.arange(4) == view_id, 1, vis_row).astype(jnp.int32)
    normed, residual = kernel_call(
        attention_kernel,
        (jax.ShapeDtypeStruct((128, 768), BF), pltpu.HBM((128, 768), F32)),
        [SMEM, SMEM, SMEM, SMEM] + [VMEM] * 6,
        scratch=[
            pltpu.VMEM((12, 768, 128), BF),
            pltpu.VMEM((128, 768), F32),
            pltpu.VMEM((128, 768), F32),
            pltpu.SemaphoreType.DMA((6,)),
        ],
        out_specs=(VMEM, HBM),
    )(
        where,
        band_start[0, 0],
        band_end[0, 0],
        seen,
        nearby,
        own,
        other,
        queries[0, 0].reshape(128, 768),
        stream[0, 0].reshape(128, 768),
        norm_gain.reshape(1, 768),
    )
    tokens = lax.all_gather(normed, "view", axis=0, tiled=True)
    tokens = kernel_call(
        swap_kernel, jax.ShapeDtypeStruct((512, 768), BF), [SMEM, VMEM]
    )(where, tokens)
    parts = kernel_call(
        mlp_kernel,
        jax.ShapeDtypeStruct((4, 128, 768), BF),
        [VMEM, VMEM],
        scratch=[pltpu.VMEM((768, 768), BF), pltpu.VMEM((768, 768), BF)],
    )(tokens, mlp)
    arrived = lax.all_to_all(parts, "view", split_axis=0, concat_axis=0, tiled=True)
    result = kernel_call(
        sum_kernel, jax.ShapeDtypeStruct((128, 768), BF), [VMEM] * 2
    )(arrived, residual)
    return result.reshape(1, 1, 4, 32, 768)


def solution(mesh):
    finer = Mesh(
        mesh.devices.reshape(mesh.shape["dp"], 2, 8, mesh.shape["view"]),
        ("dp", "slab_0", "slab_1", "view"),
    )
    in_specs = (
        P("dp", "view", SLAB, None, None),
        P(DP_SLAB, None),
        P(DP_SLAB, None),
        P("dp", "view", SLAB, None, None),
        P("dp", "view", SLAB, None, None),
        P(),
        P(DP_SLAB, "view"),
        P(DP_SLAB, "view"),
        P("dp", "view", SLAB, None),
        P("dp", "view", SLAB, None),
        P("dp", None, None),
    )
    out_specs = P("dp", "view", SLAB, None, None)
    return jax.shard_map(
        shards, mesh=finer, in_specs=in_specs, out_specs=out_specs, check_vma=False
    )
```

profile of v0, /device:TPU:1, one launch (start us, length us, event | category | flops | bytes accessed | tf_op | source)
XLA Modules:
  0.0 114.0 jit_solution(10297924364179311739)
XLA Ops:
  0.0 0.1 pad_add_fusion.where_ref
  0.1 2.1 %shard_map.109 = bf16[16,108,128]{2,1,0:T(8,128)(2,1)} custom-call(s32[2]{0:T(128)S(1)} %pad_add_fusion.where_ref, bf16[18,256]{1,0:T(8,128)(2,1)} %refs_0_.1, bf16[2,1536]{1,0:T(2,128)(2,1)} %refs_1_.1, bf16[6,768]{1,0:T(8,128)(2,1)} %refs_2_.1, bf16[6,768]{1,0:T(8,128)(2,1)} %refs_3_.1), custom_call_target="tpu_custom_call" | custom-call | tf_op jit(solution)/shard_map/pallas_call | solution.py:273
  2.2 10.2 %all-to-all-start = ((bf16[16,108,128]{2,1,0:T(8,128)(2,1)}), bf16[16,108,128]{2,1,0:T(8,128)(2,1)S(1)}, u32[]{:S(2)}, u32[]{:S(2)}) async-start(bf16[16,108,128]{2,1,0:T(8,128)(2,1)} %shard_map.109), calls=%async_computation | async-start | bytes 917504 | tf_op jit(solution)/shard_map/all_to_all | solution.py:233
  12.5 4.0 %collective-permute-start = (bf16[2,32,256]{2,1,0:T(8,128)(2,1)S(1)}, bf16[2,32,256]{2,1,0:T(8,128)(2,1)S(1)}, u32[]{:S(2)}, u32[]{:S(2)}) collective-permute-start(bf16[2,32,256]{2,1,0:T(8,128)(2,1)S(1)} %get-tuple-element.16), channel_id=1, source_target_pairs={{0,4},{4,8},{8,12},{12,16},{16,20},{20,24},{24,28},{28,32},{32,36}... | collective-permute-start | bytes 98312 | tf_op jit(solution)/shard_map/ppermute | solution.py:268
  16.5 1.3 %collective-permute-start.1 = (bf16[2,32,256]{2,1,0:T(8,128)(2,1)S(1)}, bf16[2,32,256]{2,1,0:T(8,128)(2,1)S(1)}, u32[]{:S(2)}, u32[]{:S(2)}) collective-permute-start(bf16[2,32,256]{2,1,0:T(8,128)(2,1)S(1)} %get-tuple-element.17), channel_id=1, source_target_pairs={{4,0},{8,4},{12,8},{16,12},{20,16},{24,20},{28,24},{32,28},{36,32}... | collective-permute-start | bytes 98312 | tf_op jit(solution)/shard_map/ppermute | solution.py:269
  17.8 5.6 %collective-permute-done.1 = bf16[2,32,256]{2,1,0:T(8,128)(2,1)S(1)} collective-permute-done((bf16[2,32,256]{2,1,0:T(8,128)(2,1)S(1)}, bf16[2,32,256]{2,1,0:T(8,128)(2,1)S(1)}, u32[]{:S(2)}, u32[]{:S(2)}) %collective-permute-start.1) | collective-permute-done | bytes 32800 | tf_op jit(solution)/shard_map/ppermute | solution.py:269
  23.4 0.7 pad_maximum_fusion.1
  24.1 1.3 %all-to-all-done = bf16[16,108,128]{2,1,0:T(8,128)(2,1)S(1)} async-done(((bf16[16,108,128]{2,1,0:T(8,128)(2,1)}), bf16[16,108,128]{2,1,0:T(8,128)(2,1)S(1)}, u32[]{:S(2)}, u32[]{:S(2)}) %all-to-all-start) | async-done | bytes 442400 | tf_op jit(solution)/shard_map/all_to_all | solution.py:233
  25.5 0.1 fusion
  25.5 0.1 copy.18
  25.7 0.1 reshape.39
  25.8 1.2 %broadcast_in_dim.11 = bf16[8,576,128]{2,1,0:T(8,128)(2,1)} broadcast(bf16[576,128]{1,0:T(8,128)(2,1)S(1)} %pad_select_fusion), dimensions={1,2} | broadcast | bytes 1327104 | tf_op jit(solution)/shard_map/broadcast_in_dim | solution.py:229
  27.0 9.9 %all-to-all-start.1 = ((bf16[8,576,128]{2,1,0:T(8,128)(2,1)}), bf16[8,576,128]{2,1,0:T(8,128)(2,1)S(1)}, u32[]{:S(2)}, u32[]{:S(2)}) async-start(bf16[8,576,128]{2,1,0:T(8,128)(2,1)} %broadcast_in_dim.11), calls=%async_computation.1 | async-start | bytes 2359296 | tf_op jit(solution)/shard_map/all_to_all | solution.py:233
  36.9 0.1 copy.20
  37.0 0.1 reshape.44
  37.1 0.1 copy.22
  37.1 0.1 reshape.46
  37.2 19.2 %all-to-all-done.1.own_ref = bf16[8,576,128]{2,1,0:T(8,128)(2,1)S(1)} async-done(((bf16[8,576,128]{2,1,0:T(8,128)(2,1)}), bf16[8,576,128]{2,1,0:T(8,128)(2,1)S(1)}, u32[]{:S(2)}, u32[]{:S(2)}) %all-to-all-start.1) | async-done | bytes 1179680 | tf_op jit(solution)/shard_map/all_to_all | solution.py:233
  56.4 1.7 %broadcast_in_dim.12 = bf16[8,1152,128]{2,1,0:T(8,128)(2,1)} broadcast(bf16[1152,128]{1,0:T(8,128)(2,1)S(1)} %pad_maximum_fusion), dimensions={1,2} | broadcast | bytes 2654208 | tf_op jit(solution)/shard_map/broadcast_in_dim | solution.py:229
  58.1 3.7 %all-to-all-start.2 = ((bf16[8,1152,128]{2,1,0:T(8,128)(2,1)}), bf16[8,1152,128]{2,1,0:T(8,128)(2,1)S(1)}, u32[]{:S(2)}, u32[]{:S(2)}) async-start(bf16[8,1152,128]{2,1,0:T(8,128)(2,1)} %broadcast_in_dim.12), calls=%async_computation.2 | async-start | bytes 4718592 | tf_op jit(solution)/shard_map/all_to_all | solution.py:233
  61.9 3.7 %collective-permute-start.2 = (bf16[8,576,128]{2,1,0:T(8,128)(2,1)S(1)}, bf16[8,576,128]{2,1,0:T(8,128)(2,1)}, u32[]{:S(2)}, u32[]{:S(2)}) collective-permute-start(bf16[8,576,128]{2,1,0:T(8,128)(2,1)S(1)} %all-to-all-done.1.own_ref), channel_id=1, source_target_pairs={{0,1},{1,0},{2,3},{3,2},{4,5},{5,4},{6,7},{7,6},{8,9},{9,8},{10,11... | collective-permute-start | bytes 3538952 | tf_op jit(solution)/shard_map/ppermute | solution.py:291
  65.6 0.7 compare_select_fusion.seen_ref
  66.3 1.8 %collective-permute-done.2.other_ref = bf16[8,576,128]{2,1,0:T(8,128)(2,1)} collective-permute-done((bf16[8,576,128]{2,1,0:T(8,128)(2,1)S(1)}, bf16[8,576,128]{2,1,0:T(8,128)(2,1)}, u32[]{:S(2)}, u32[]{:S(2)}) %collective-permute-start.2) | collective-permute-done | bytes 1179680 | tf_op jit(solution)/shard_map/ppermute | solution.py:291
  68.2 2.8 %shard_map.110 = bf16[192,256]{1,0:T(8,128)(2,1)S(1)} custom-call(s32[2]{0:T(128)S(1)} %pad_add_fusion.where_ref, bf16[256,256]{1,0:T(8,128)(2,1)} %bitcast.35, bf16[8,576,128]{2,1,0:T(8,128)(2,1)S(1)} %all-to-all-done.1.own_ref, bf16[8,576,128]{2,1,0:T(8,128)(2,1)} %collective-permute-done.2.other_ref), custom_call_target="tpu_custom_call" | custom-call | tf_op jit(solution)/shard_map/pallas_call | solution.py:294
  70.9 6.6 %all_gather.6.enc_ref = bf16[768,256]{1,0:T(8,128)(2,1)S(1)} all-gather(bf16[192,256]{1,0:T(8,128)(2,1)S(1)} %shard_map.110), channel_id=1, replica_groups=mesh['dp'=8,'slab_0'=2,'slab_1'=8,'view'=4] {'view'}, dimensions={0}, use_global_device_ids=true | all-gather | bytes 491520 | tf_op jit(solution)/shard_map/all_gather | solution.py:304
  77.5 6.0 %shard_map.111 = (bf16[128,768]{1,0:T(8,128)(2,1)S(1)}, f32[128,768]{1,0:T(8,128)}) custom-call(s32[2]{0:T(128)S(1)} %pad_add_fusion.where_ref, s32[4,4]{1,0:T(4,128)S(1)} %bitcast.30, s32[4,4]{1,0:T(4,128)S(1)} %bitcast.31, s32[4]{0:T(128)S(1)} %compare_select_fusion.seen_ref, bf16[768,256]{1,0:T(8,128)(2,1)S(1)} %all_gather.6.enc_ref, ...), custom_call_target="tpu_custom_call" | custom-call | tf_op jit(solution)/shard_map/pallas_call | solution.py:307
  83.6 8.7 %all_gather.7.tok_ref = bf16[512,768]{1,0:T(8,128)(2,1)S(1)} all-gather(bf16[128,768]{1,0:T(8,128)(2,1)S(1)} %get-tuple-element.11), channel_id=1, replica_groups=mesh['dp'=8,'slab_0'=2,'slab_1'=8,'view'=4] {'view'}, dimensions={0}, use_global_device_ids=true | all-gather | bytes 983040 | tf_op jit(solution)/shard_map/all_gather | solution.py:330
  92.3 1.4 %shard_map.112.tok_ref = bf16[512,768]{1,0:T(8,128)(2,1)S(1)} custom-call(s32[2]{0:T(128)S(1)} %pad_add_fusion.where_ref, bf16[512,768]{1,0:T(8,128)(2,1)S(1)} %all_gather.7.tok_ref), custom_call_target="tpu_custom_call" | custom-call | tf_op jit(solution)/shard_map/pallas_call | solution.py:331
  93.7 0.3 all-to-all-done.2.w_ref
  93.9 2.5 %shard_map.113 = bf16[4,128,768]{2,1,0:T(8,128)(2,1)S(1)} custom-call(bf16[512,768]{1,0:T(8,128)(2,1)S(1)} %shard_map.112.tok_ref, bf16[8,1152,128]{2,1,0:T(8,128)(2,1)S(1)} %all-to-all-done.2.w_ref), custom_call_target="tpu_custom_call" | custom-call | tf_op jit(solution)/shard_map/pallas_call | solution.py:334
  96.5 15.8 %all_to_all.20.parts_ref = bf16[4,128,768]{2,1,0:T(8,128)(2,1)S(1)} all-to-all(bf16[4,128,768]{2,1,0:T(8,128)(2,1)S(1)} %shard_map.113), channel_id=1, replica_groups=mesh['dp'=8,'slab_0'=2,'slab_1'=8,'view'=4] {'view'}, dimensions={0} | all-to-all | bytes 1572864 | tf_op jit(solution)/shard_map/all_to_all | solution.py:340
  112.3 1.7 %shard_map.114 = bf16[128,768]{1,0:T(8,128)(2,1)} custom-call(bf16[4,128,768]{2,1,0:T(8,128)(2,1)S(1)} %all_to_all.20.parts_ref, f32[128,768]{1,0:T(8,128)S(1)} %copy-done), custom_call_target="tpu_custom_call" | custom-call | tf_op jit(solution)/shard_map/pallas_call | solution.py:341
  (24 shorter events, 0.2 us)
Async XLA Ops:
  0.0 12.5 %copy-start.5 = (bf16[1,1,4,32,256]{4,3,2,1,0:T(8,128)(2,1)S(1)}, bf16[1,1,4,32,256]{4,3,2,1,0:T(8,128)(2,1)}, u32[]{:S(2)}) copy-start(bf16[1,1,4,32,256]{4,3,2,1,0:T(8,128)(2,1)} %param.11) | copy-start | bytes 196612
  2.2 23.2 %all-to-all-start = ((bf16[16,108,128]{2,1,0:T(8,128)(2,1)}), bf16[16,108,128]{2,1,0:T(8,128)(2,1)S(1)}, u32[]{:S(2)}, u32[]{:S(2)}) async-start(bf16[16,108,128]{2,1,0:T(8,128)(2,1)} %shard_map.109), calls=%async_computation | async-start | bytes 917504 | tf_op jit(solution)/shard_map/all_to_all | solution.py:233
  12.5 5.3 %collective-permute-start = (bf16[2,32,256]{2,1,0:T(8,128)(2,1)S(1)}, bf16[2,32,256]{2,1,0:T(8,128)(2,1)S(1)}, u32[]{:S(2)}, u32[]{:S(2)}) collective-permute-start(bf16[2,32,256]{2,1,0:T(8,128)(2,1)S(1)} %get-tuple-element.16), channel_id=1, source_target_pairs={{0,4},{4,8},{8,12},{12,16},{16,20},{20,24},{24,28},{28,32},{32,36}... | collective-permute-start | bytes 98312 | tf_op jit(solution)/shard_map/ppermute | solution.py:268
  16.5 7.0 %collective-permute-start.1 = (bf16[2,32,256]{2,1,0:T(8,128)(2,1)S(1)}, bf16[2,32,256]{2,1,0:T(8,128)(2,1)S(1)}, u32[]{:S(2)}, u32[]{:S(2)}) collective-permute-start(bf16[2,32,256]{2,1,0:T(8,128)(2,1)S(1)} %get-tuple-element.17), channel_id=1, source_target_pairs={{4,0},{8,4},{12,8},{16,12},{20,16},{24,20},{28,24},{32,28},{36,32}... | collective-permute-start | bytes 98312 | tf_op jit(solution)/shard_map/ppermute | solution.py:269
  27.0 29.4 %all-to-all-start.1 = ((bf16[8,576,128]{2,1,0:T(8,128)(2,1)}), bf16[8,576,128]{2,1,0:T(8,128)(2,1)S(1)}, u32[]{:S(2)}, u32[]{:S(2)}) async-start(bf16[8,576,128]{2,1,0:T(8,128)(2,1)} %broadcast_in_dim.11), calls=%async_computation.1 | async-start | bytes 2359296 | tf_op jit(solution)/shard_map/all_to_all | solution.py:233
  58.1 7.5 %copy-start.6 = (f32[768]{0:T(1024)S(1)}, f32[768]{0:T(1024)}, u32[]{:S(2)}) copy-start(f32[768]{0:T(1024)} %param.16) | copy-start | bytes 9220
  58.1 35.8 %all-to-all-start.2 = ((bf16[8,1152,128]{2,1,0:T(8,128)(2,1)}), bf16[8,1152,128]{2,1,0:T(8,128)(2,1)S(1)}, u32[]{:S(2)}, u32[]{:S(2)}) async-start(bf16[8,1152,128]{2,1,0:T(8,128)(2,1)} %broadcast_in_dim.12), calls=%async_computation.2 | async-start | bytes 4718592 | tf_op jit(solution)/shard_map/all_to_all | solution.py:233
  61.9 6.3 %collective-permute-start.2 = (bf16[8,576,128]{2,1,0:T(8,128)(2,1)S(1)}, bf16[8,576,128]{2,1,0:T(8,128)(2,1)}, u32[]{:S(2)}, u32[]{:S(2)}) collective-permute-start(bf16[8,576,128]{2,1,0:T(8,128)(2,1)S(1)} %all-to-all-done.1.own_ref), channel_id=1, source_target_pairs={{0,1},{1,0},{2,3},{3,2},{4,5},{5,4},{6,7},{7,6},{8,9},{9,8},{10,11... | collective-permute-start | bytes 3538952 | tf_op jit(solution)/shard_map/ppermute | solution.py:291
  66.3 11.2 %copy-start.1 = (bf16[1,1,4,32,768]{4,3,2,1,0:T(8,128)(2,1)S(1)}, bf16[1,1,4,32,768]{4,3,2,1,0:T(8,128)(2,1)}, u32[]{:S(2)}) copy-start(bf16[1,1,4,32,768]{4,3,2,1,0:T(8,128)(2,1)} %param.15) | copy-start | bytes 589828
  66.3 11.2 %copy-start.2 = (bf16[1,1,4,32,768]{4,3,2,1,0:T(8,128)(2,1)S(1)}, bf16[1,1,4,32,768]{4,3,2,1,0:T(8,128)(2,1)}, u32[]{:S(2)}) copy-start(bf16[1,1,4,32,768]{4,3,2,1,0:T(8,128)(2,1)} %param.14) | copy-start | bytes 589828
  66.3 11.2 %copy-start.3 = (s32[1,1,4,4]{3,2,1,0:T(4,128)S(1)}, s32[1,1,4,4]{3,2,1,0:T(4,128)}, u32[]{:S(2)}) copy-start(s32[1,1,4,4]{3,2,1,0:T(4,128)} %param.19) | copy-start | bytes 196
  66.3 11.2 %copy-start.4 = (s32[1,1,4,4]{3,2,1,0:T(4,128)S(1)}, s32[1,1,4,4]{3,2,1,0:T(4,128)}, u32[]{:S(2)}) copy-start(s32[1,1,4,4]{3,2,1,0:T(4,128)} %param.20) | copy-start | bytes 196
  96.5 15.8 %copy-start = (f32[128,768]{1,0:T(8,128)S(1)}, f32[128,768]{1,0:T(8,128)}, u32[]{:S(2)}) copy-start(f32[128,768]{1,0:T(8,128)} %get-tuple-element.12.residual_ref) | copy-start | bytes 1179652
where the time goes:
time: 115 us; the launch traced here: 114 us
  starting transfers between devices  32.8 us (29%)
  blocking collectives  31.1 us (27%)
  waiting for transfers between devices  28.3 us (25%)
  Pallas kernels  16.6 us (14%)
  local copies, waits for them, and re-layouts  3.51 us (3%)
  other arithmetic  1.5 us (1%)
    all_to_all x3, starting transfers between devices, exchange(): lax.all_to_all(copies, ('dp', 'slab_0', 'slab_1', 'view'), split_axis=0,...  23.8 us
    all_to_all x3, waiting for transfers between devices, exchange(): lax.all_to_all(copies, ('dp', 'slab_0', 'slab_1', 'view'), split_axis=0,...  20.8 us
    all_to_all x1, blocking collectives, shards(): lax.all_to_all(parts, 'view', split_axis=0, concat_axis=0, tiled=True)  15.8 us
    all_gather x1, blocking collectives, shards(): tokens = lax.all_gather(normed, 'view', axis=0, tiled=True)  8.71 us
    all_gather x1, blocking collectives, shards(): nearby = lax.all_gather(encoded, 'view', axis=0, tiled=True)  6.57 us
    pallas_call x1, Pallas kernels, shards(): kernel_call(attention_kernel, (jax.ShapeDtypeStruct((128, 768), BF), pltp...  6.04 us
    ppermute x1, waiting for transfers between devices, shards(): below = lax.ppermute(feats[:2], SLAB, [(i + 1, i) for i in range(ends)])  5.64 us
    ppermute x1, starting transfers between devices, shards(): above = lax.ppermute(feats[2:], SLAB, [(i, i + 1) for i in range(ends)])  4 us
  transfers between devices with their start and end apart: 6, of which 5 were waited for; matrix products, arithmetic and copies ran while one was open for 1% of the time, Pallas kernels for 9%

commit v1 on v0

--- a/solution.py
+++ b/solution.py
@@ -27,34 +27,40 @@
     return jnp.where(here == row, 1.0, 0.0).astype(BF)
 
 
-def conv_kernel(where_ref, rows_ref, own_ref, other_ref, out_ref, x_ref, weight_ref, sem):
+def conv_kernel(where_ref, rows_ref, own_ref, other_ref, out_ref, x_ref, sem):
     copy = pltpu.make_async_copy(rows_ref, x_ref, sem)
     copy.start()
-    for core, ref in ((0, own_ref), (1, other_ref)):
-
-        @pl.when(where_ref[0] == core)
-        def _(ref=ref):
-            for tile in range(2):
-                cols = slice(tile * 128, (tile + 1) * 128)
-                for d in range(8):
-                    rows = slice(d * 288, (d + 1) * 288)
-                    weight_ref[rows, cols] = ref[d, tile * 288 : (tile + 1) * 288, :]
-
     copy.wait()
     x = x_ref[...].astype(F32)
     col = lax.broadcasted_iota(jnp.int32, x.shape, 0) % 32
     left = jnp.where(col == 0, 0.0, pltpu.roll(x, 1, 0)).astype(BF)
     right = jnp.where(col == 31, 0.0, pltpu.roll(x, x.shape[0] - 1, 0)).astype(BF)
     shifted = (left, x_ref[...], right)
-    conv = jnp.zeros((192, 256), F32)
-    for tap in range(9):
-        rows = shifted[tap % 3][tap // 3 * 32 : tap // 3 * 32 + 192]
-        conv = conv + jnp.dot(
-            rows, weight_ref[tap * 256 : (tap + 1) * 256, :], preferred_element_type=F32
-        )
-    silu = conv / (1.0 + jnp.exp(-conv))
-    encoded = (x[32:224] + silu).astype(BF)
-    out_ref[...] = jnp.dot(encoded, one_hot(256, 2), preferred_element_type=F32).astype(BF)
+    swap = one_hot(256, 2)
+
+    def tap_weight(ref, tap):
+        tiles = []
+        for tile in range(2):
+            at, end, pieces = tap * 256, (tap + 1) * 256, []
+            while at < end:
+                d, low = divmod(at, 288)
+                high = min(288, low + end - at)
+                pieces.append(ref[d, tile * 288 + low : tile * 288 + high, :])
+                at += high - low
+            tiles.append(pieces[0] if len(pieces) == 1 else jnp.concatenate(pieces, axis=0))
+        return jnp.concatenate(tiles, axis=1)
+
+    for core, ref in ((0, own_ref), (1, other_ref)):
+
+        @pl.when(where_ref[0] == core)
+        def _(ref=ref):
+            conv = jnp.zeros((192, 256), F32)
+            for tap in range(9):
+                rows = shifted[tap % 3][tap // 3 * 32 : tap // 3 * 32 + 192]
+                conv = conv + jnp.dot(rows, tap_weight(ref, tap), preferred_element_type=F32)
+            silu = conv / (1.0 + jnp.exp(-conv))
+            encoded = (x[32:224] + silu).astype(BF)
+            out_ref[...] = jnp.dot(encoded, swap, preferred_element_type=F32).astype(BF)
 
 
 def attention_kernel(
@@ -78,12 +84,20 @@
     first = where_ref[0] == 0
     first_row = where_ref[1]
     enc = enc_ref[...]
-    for tile in range(12):
-        at = slice(tile * 32, (tile + 1) * 32)
-        weight = jnp.concatenate(
-            [jnp.where(first, other_ref[z, at, :], own_ref[z, at, :]) for z in range(8)], axis=0
-        )
-        kv_ref[tile] = jnp.dot(enc, weight, preferred_element_type=F32).astype(BF)
+    for couple in range(6):
+        tiles = []
+        for tile in (2 * couple, 2 * couple + 1):
+            at = slice(tile * 32, (tile + 1) * 32)
+            tiles.append(
+                jnp.concatenate(
+                    [jnp.where(first, other_ref[z, at, :], own_ref[z, at, :]) for z in range(8)],
+                    axis=0,
+                )
+            )
+        weight = jnp.concatenate(tiles, axis=1)
+        kv = jnp.dot(enc, weight, preferred_element_type=F32).astype(BF)
+        kv_ref[2 * couple] = kv[:, :128]
+        kv_ref[2 * couple + 1] = kv[:, 128:]
     lane = lax.broadcasted_iota(jnp.int32, (1, 768), 1)
     key_view = lane // 192
     key_row = first_row - 1 + (lane % 192) // 32
@@ -132,18 +146,27 @@
     return 0.5 * v * (1.0 + jnp.tanh(0.7978845608028654 * (v + 0.044715 * (v * v * v))))
 
 
-def mlp_kernel(tok_ref, w_ref, out_ref, up_ref, down_ref):
+def two_blocks(where_ref, tok_ref, up_ref, down_ref, out_refs, chip_flip):
+    view = where_ref[2]
+    for out_ref, flip in zip(out_refs, (0, 1)):
+        rows = pl.ds(pl.multiple_of((view ^ (chip_flip * 2 + flip)) * 128, 128), 128)
+        hidden = gelu(jnp.dot(tok_ref[rows, :], up_ref[...], preferred_element_type=F32)).astype(BF)
+        out_ref[...] = last_dims(hidden, down_ref[...]).astype(BF)
+
+
+def far_kernel(where_ref, tok_ref, w_ref, same_ref, cross_ref, up_ref, down_ref):
     for tile in range(6):
         cols = slice(tile * 128, (tile + 1) * 128)
         for d in range(8):
             rows = slice(d * 96, (d + 1) * 96)
             up_ref[rows, cols] = w_ref[d, tile * 96 : (tile + 1) * 96, :]
             down_ref[rows, cols] = w_ref[d, 576 + tile * 96 : 576 + (tile + 1) * 96, :]
-
-    for block in range(4):
-        tokens = tok_ref[block * 128 : (block + 1) * 128, :]
-        hidden = gelu(jnp.dot(tokens, up_ref[...], preferred_element_type=F32)).astype(BF)
-        out_ref[block] = last_dims(hidden, down_ref[...]).astype(BF)
+    two_blocks(where_ref, tok_ref, up_ref, down_ref, (same_ref, cross_ref), 1)
+
+
+def near_kernel(where_ref, tok_ref, up_ref, down_ref, own_ref, sibling_ref, swap_ref):
+    two_blocks(where_ref, tok_ref, up_ref, down_ref, (own_ref, sibling_ref), 0)
+    swap_ref[...] = one_hot(768, 6)
 
 
 def swap_kernel(where_ref, tok_ref, out_ref):
@@ -156,13 +179,17 @@
         out_ref[...] = jnp.dot(tok_ref[...], one_hot(768, 6), preferred_element_type=F32).astype(BF)
 
 
-def sum_kernel(parts_ref, residual_ref, out_ref):
-    swap = one_hot(768, 6)
-    odd = parts_ref[1].astype(F32) + parts_ref[3].astype(F32)
+def sum_kernel(
+    where_ref, own_ref, sibling_ref, same_ref, cross_ref, swap_ref, residual_ref, out_ref
+):
+    alike = own_ref[...].astype(F32) + same_ref[...].astype(F32)
+    unlike = sibling_ref[...].astype(F32) + cross_ref[...].astype(F32)
+    first = where_ref[0] == 0
+    odd = jnp.where(first, unlike, alike)
+    even = jnp.where(first, alike, unlike)
     high = odd.astype(BF)
     low = (odd - high.astype(F32)).astype(BF)
-    odd = last_dims(high, swap) + last_dims(low, swap)
-    even = parts_ref[0].astype(F32) + parts_ref[2].astype(F32)
+    odd = last_dims(high, swap_ref[...]) + last_dims(low, swap_ref[...])
     out_ref[...] = (residual_ref[...] + (even + odd)).astype(BF)
 
 
@@ -223,6 +250,10 @@
             lines = ids[..., view].transpose(*held, *axes)
             groups.extend(lines.reshape(-1, int(np.prod([ids.shape[a] for a in axes]))).tolist())
     return groups
+
+
+def to_view(value, flip):
+    return lax.ppermute(value, "view", [(i, i ^ flip) for i in range(4)])
 
 
 def copies_of(value, count):
@@ -262,7 +293,7 @@
     view_id = lax.axis_index("view")
     core = view_id % 2
     first_row = lax.axis_index(SLAB) * 4
-    where = jnp.stack([core, first_row]).astype(jnp.int32)
+    where = jnp.stack([core, first_row, view_id]).astype(jnp.int32)
     feats = latent_feats[0, 0]
     ends = lax.axis_size(SLAB) - 1
     above = lax.ppermute(feats[2:], SLAB, [(i, i + 1) for i in range(ends)])
@@ -288,7 +319,7 @@
     code = copies_of(code, 8)
     own = exchange(code, long)
     units = copies_of(units, 8)
-    other = lax.ppermute(own, "view", [(i, i ^ 1) for i in range(4)])
+    other = to_view(own, 1)
     mlp = exchange(units, long)
 
     encoded = kernel_call(
@@ -297,7 +328,6 @@
         [SMEM, HBM, VMEM, VMEM],
         scratch=[
             pltpu.VMEM((256, 256), BF),
-            pltpu.VMEM((2304, 256), BF),
             pltpu.SemaphoreType.DMA(()),
         ],
     )(where, in_hbm(rows), own, other)
@@ -331,16 +361,20 @@
     tokens = kernel_call(
         swap_kernel, jax.ShapeDtypeStruct((512, 768), BF), [SMEM, VMEM]
     )(where, tokens)
-    parts = kernel_call(
-        mlp_kernel,
-        jax.ShapeDtypeStruct((4, 128, 768), BF),
-        [VMEM, VMEM],
-        scratch=[pltpu.VMEM((768, 768), BF), pltpu.VMEM((768, 768), BF)],
-    )(tokens, mlp)
-    arrived = lax.all_to_all(parts, "view", split_axis=0, concat_axis=0, tiled=True)
+    block = jax.ShapeDtypeStruct((128, 768), BF)
+    square = jax.ShapeDtypeStruct((768, 768), BF)
+    same, cross, up, down = kernel_call(
+        far_kernel, (block, block, square, square), [SMEM, VMEM, VMEM]
+    )(where, tokens, mlp)
+    cross = to_view(cross, 3)
+    same = to_view(same, 2)
+    own, sibling, swap = kernel_call(
+        near_kernel, (block, block, square), [SMEM] + [VMEM] * 3
+    )(where, tokens, up, down)
+    sibling = to_view(sibling, 1)
     result = kernel_call(
-        sum_kernel, jax.ShapeDtypeStruct((128, 768), BF), [VMEM] * 2
-    )(arrived, residual)
+        sum_kernel, block, [SMEM] + [VMEM] * 6
+    )(where, own, sibling, same, cross, swap, residual)
     return result.reshape(1, 1, 4, 32, 768)
 
 

time: 115 us -> 119 us (1.035)
  blocking collectives: 31.1 us -> 15.3 us
  starting transfers between devices: 32.8 us -> 42.9 us
  waiting for transfers between devices: 28.3 us -> 35.9 us
  Pallas kernels: 16.6 us -> 18.5 us
    all_to_all x1 -> x0, blocking collectives: 15.8 us -> none  [shards(): lax.all_to_all(parts, 'view', split_axis=0, concat_axis=0, tiled=True)]
    ppermute x1 -> x4, starting transfers between devices: 3.69 us -> 13.7 us  [to_view(): return lax.ppermute(value, 'view', [(i, i ^ flip) for i in range(4)])]
    ppermute x1 -> x4, waiting for transfers between devices: 1.84 us -> 9.09 us  [to_view(): return lax.ppermute(value, 'view', [(i, i ^ flip) for i in range(4)])]
    pallas_call x2 -> x3, Pallas kernels: 4.24 us -> 6.58 us  [the longest x1 2.39 us: shards(): kernel_call(near_kernel, (block, block, square), [SMEM] + [VMEM] * 3)]
  transfers between devices with their start and end apart: 6 -> 9, of which waited for: 5 -> 7; matrix products, arithmetic and copies ran while one was open for 1% -> 1% of each run, Pallas kernels for 9% -> 8%
where the time goes in v1:
time: 119 us; the launch traced here: 118 us
  starting transfers between devices  42.9 us (36%)
  waiting for transfers between devices  35.9 us (30%)
  Pallas kernels  18.5 us (16%)
  blocking collectives  15.3 us (13%)
  local copies, waits for them, and re-layouts  3.5 us (3%)
  other arithmetic  1.5 us (1%)
    all_to_all x3, starting transfers between devices, exchange(): lax.all_to_all(copies, ('dp', 'slab_0', 'slab_1', 'view'), split_axis=0,...  23.8 us
    all_to_all x3, waiting for transfers between devices, exchange(): lax.all_to_all(copies, ('dp', 'slab_0', 'slab_1', 'view'), split_axis=0,...  21.2 us
    ppermute x4, starting transfers between devices, to_view(): return lax.ppermute(value, 'view', [(i, i ^ flip) for i in range(4)])  13.7 us
    ppermute x4, waiting for transfers between devices, to_view(): return lax.ppermute(value, 'view', [(i, i ^ flip) for i in range(4)])  9.09 us
    all_gather x1, blocking collectives, shards(): tokens = lax.all_gather(normed, 'view', axis=0, tiled=True)  8.71 us
    all_gather x1, blocking collectives, shards(): nearby = lax.all_gather(encoded, 'view', axis=0, tiled=True)  6.57 us
    ppermute x1, waiting for transfers between devices, shards(): below = lax.ppermute(feats[:2], SLAB, [(i + 1, i) for i in range(ends)])  5.64 us
    pallas_call x1, Pallas kernels, shards(): kernel_call(attention_kernel, (jax.ShapeDtypeStruct((128, 768), BF), pltp...  5.51 us
  transfers between devices with their start and end apart: 9, of which 7 were waited for; matrix products, arithmetic and copies ran while one was open for 1% of the time, Pallas kernels for 8%

profile of v1, /device:TPU:1, one launch (start us, length us, event | category | flops | bytes accessed | tf_op | source)
XLA Modules:
  0.0 117.9 jit_solution(12869280030341661940)
XLA Ops:
  0.0 0.1 pad_add_fusion.where_ref
  0.1 2.1 %shard_map.109 = bf16[16,108,128]{2,1,0:T(8,128)(2,1)} custom-call(s32[3]{0:T(128)S(1)} %pad_add_fusion.where_ref, bf16[18,256]{1,0:T(8,128)(2,1)} %refs_0_.1, bf16[2,1536]{1,0:T(2,128)(2,1)} %refs_1_.1, bf16[6,768]{1,0:T(8,128)(2,1)} %refs_2_.1, bf16[6,768]{1,0:T(8,128)(2,1)} %refs_3_.1), custom_call_target="tpu_custom_call" | custom-call | tf_op jit(solution)/shard_map/pallas_call | solution.py:304
  2.2 10.2 %all-to-all-start = ((bf16[16,108,128]{2,1,0:T(8,128)(2,1)}), bf16[16,108,128]{2,1,0:T(8,128)(2,1)S(1)}, u32[]{:S(2)}, u32[]{:S(2)}) async-start(bf16[16,108,128]{2,1,0:T(8,128)(2,1)} %shard_map.109), calls=%async_computation | async-start | bytes 917504 | tf_op jit(solution)/shard_map/all_to_all | solution.py:264
  12.5 4.0 %collective-permute-start = (bf16[2,32,256]{2,1,0:T(8,128)(2,1)S(1)}, bf16[2,32,256]{2,1,0:T(8,128)(2,1)S(1)}, u32[]{:S(2)}, u32[]{:S(2)}) collective-permute-start(bf16[2,32,256]{2,1,0:T(8,128)(2,1)S(1)} %get-tuple-element.30), channel_id=1, source_target_pairs={{0,4},{4,8},{8,12},{12,16},{16,20},{20,24},{24,28},{28,32},{32,36}... | collective-permute-start | bytes 98312 | tf_op jit(solution)/shard_map/ppermute | solution.py:299
  16.5 1.3 %collective-permute-start.1 = (bf16[2,32,256]{2,1,0:T(8,128)(2,1)S(1)}, bf16[2,32,256]{2,1,0:T(8,128)(2,1)S(1)}, u32[]{:S(2)}, u32[]{:S(2)}) collective-permute-start(bf16[2,32,256]{2,1,0:T(8,128)(2,1)S(1)} %get-tuple-element.31), channel_id=1, source_target_pairs={{4,0},{8,4},{12,8},{16,12},{20,16},{24,20},{28,24},{32,28},{36,32}... | collective-permute-start | bytes 98312 | tf_op jit(solution)/shard_map/ppermute | solution.py:300
  17.8 5.6 %collective-permute-done.1 = bf16[2,32,256]{2,1,0:T(8,128)(2,1)S(1)} collective-permute-done((bf16[2,32,256]{2,1,0:T(8,128)(2,1)S(1)}, bf16[2,32,256]{2,1,0:T(8,128)(2,1)S(1)}, u32[]{:S(2)}, u32[]{:S(2)}) %collective-permute-start.1) | collective-permute-done | bytes 32800 | tf_op jit(solution)/shard_map/ppermute | solution.py:300
  23.4 0.7 pad_maximum_fusion.1
  24.1 1.3 %all-to-all-done = bf16[16,108,128]{2,1,0:T(8,128)(2,1)S(1)} async-done(((bf16[16,108,128]{2,1,0:T(8,128)(2,1)}), bf16[16,108,128]{2,1,0:T(8,128)(2,1)S(1)}, u32[]{:S(2)}, u32[]{:S(2)}) %all-to-all-start) | async-done | bytes 442400 | tf_op jit(solution)/shard_map/all_to_all | solution.py:264
  25.5 0.1 fusion
  25.5 0.1 copy.18
  25.8 1.2 %broadcast_in_dim.11 = bf16[8,576,128]{2,1,0:T(8,128)(2,1)} broadcast(bf16[576,128]{1,0:T(8,128)(2,1)S(1)} %pad_select_fusion), dimensions={1,2} | broadcast | bytes 1327104 | tf_op jit(solution)/shard_map/broadcast_in_dim | solution.py:260
  27.0 9.9 %all-to-all-start.1 = ((bf16[8,576,128]{2,1,0:T(8,128)(2,1)}), bf16[8,576,128]{2,1,0:T(8,128)(2,1)S(1)}, u32[]{:S(2)}, u32[]{:S(2)}) async-start(bf16[8,576,128]{2,1,0:T(8,128)(2,1)} %broadcast_in_dim.11), calls=%async_computation.1 | async-start | bytes 2359296 | tf_op jit(solution)/shard_map/all_to_all | solution.py:264
  37.2 19.2 %all-to-all-done.1.own_ref = bf16[8,576,128]{2,1,0:T(8,128)(2,1)S(1)} async-done(((bf16[8,576,128]{2,1,0:T(8,128)(2,1)}), bf16[8,576,128]{2,1,0:T(8,128)(2,1)S(1)}, u32[]{:S(2)}, u32[]{:S(2)}) %all-to-all-start.1) | async-done | bytes 1179680 | tf_op jit(solution)/shard_map/all_to_all | solution.py:264
  56.4 1.7 %broadcast_in_dim.12 = bf16[8,1152,128]{2,1,0:T(8,128)(2,1)} broadcast(bf16[1152,128]{1,0:T(8,128)(2,1)S(1)} %pad_maximum_fusion), dimensions={1,2} | broadcast | bytes 2654208 | tf_op jit(solution)/shard_map/broadcast_in_dim | solution.py:260
  58.1 3.7 %all-to-all-start.2 = ((bf16[8,1152,128]{2,1,0:T(8,128)(2,1)}), bf16[8,1152,128]{2,1,0:T(8,128)(2,1)S(1)}, u32[]{:S(2)}, u32[]{:S(2)}) async-start(bf16[8,1152,128]{2,1,0:T(8,128)(2,1)} %broadcast_in_dim.12), calls=%async_computation.2 | async-start | bytes 4718592 | tf_op jit(solution)/shard_map/all_to_all | solution.py:264
  61.9 3.7 %collective-permute-start.2 = (bf16[8,576,128]{2,1,0:T(8,128)(2,1)S(1)}, bf16[8,576,128]{2,1,0:T(8,128)(2,1)}, u32[]{:S(2)}, u32[]{:S(2)}) collective-permute-start(bf16[8,576,128]{2,1,0:T(8,128)(2,1)S(1)} %all-to-all-done.1.own_ref), channel_id=1, source_target_pairs={{0,1},{1,0},{2,3},{3,2},{4,5},{5,4},{6,7},{7,6},{8,9},{9,8},{10,11... | collective-permute-start | bytes 3538952 | tf_op jit(solution)/shard_map/ppermute | solution.py:256
  65.6 0.7 compare_select_fusion.seen_ref
  66.3 1.8 %collective-permute-done.2.other_ref = bf16[8,576,128]{2,1,0:T(8,128)(2,1)} collective-permute-done((bf16[8,576,128]{2,1,0:T(8,128)(2,1)S(1)}, bf16[8,576,128]{2,1,0:T(8,128)(2,1)}, u32[]{:S(2)}, u32[]{:S(2)}) %collective-permute-start.2) | collective-permute-done | bytes 1179680 | tf_op jit(solution)/shard_map/ppermute | solution.py:256
  68.1 2.9 %shard_map.110 = bf16[192,256]{1,0:T(8,128)(2,1)S(1)} custom-call(s32[3]{0:T(128)S(1)} %pad_add_fusion.where_ref, bf16[256,256]{1,0:T(8,128)(2,1)} %bitcast.36, bf16[8,576,128]{2,1,0:T(8,128)(2,1)S(1)} %all-to-all-done.1.own_ref, bf16[8,576,128]{2,1,0:T(8,128)(2,1)} %collective-permute-done.2.other_ref), custom_call_target="tpu_custom_call" | custom-call | tf_op jit(solution)/shard_map/pallas_call | solution.py:325
  71.0 6.6 %all_gather.6.enc_ref = bf16[768,256]{1,0:T(8,128)(2,1)S(1)} all-gather(bf16[192,256]{1,0:T(8,128)(2,1)S(1)} %shard_map.110), channel_id=1, replica_groups=mesh['dp'=8,'slab_0'=2,'slab_1'=8,'view'=4] {'view'}, dimensions={0}, use_global_device_ids=true | all-gather | bytes 491520 | tf_op jit(solution)/shard_map/all_gather | solution.py:334
  77.6 5.5 %shard_map.111 = (bf16[128,768]{1,0:T(8,128)(2,1)S(1)}, f32[128,768]{1,0:T(8,128)}) custom-call(s32[3]{0:T(128)S(1)} %pad_add_fusion.where_ref, s32[4,4]{1,0:T(4,128)S(1)} %bitcast.31, s32[4,4]{1,0:T(4,128)S(1)} %bitcast.32, s32[4]{0:T(128)S(1)} %compare_select_fusion.seen_ref, bf16[768,256]{1,0:T(8,128)(2,1)S(1)} %all_gather.6.enc_ref, ...), custom_call_target="tpu_custom_call" | custom-call | tf_op jit(solution)/shard_map/pallas_call | solution.py:337
  83.1 8.7 %all_gather.7.tok_ref = bf16[512,768]{1,0:T(8,128)(2,1)S(1)} all-gather(bf16[128,768]{1,0:T(8,128)(2,1)S(1)} %get-tuple-element.18), channel_id=1, replica_groups=mesh['dp'=8,'slab_0'=2,'slab_1'=8,'view'=4] {'view'}, dimensions={0}, use_global_device_ids=true | all-gather | bytes 983040 | tf_op jit(solution)/shard_map/all_gather | solution.py:360
  91.8 1.4 %shard_map.112.tok_ref = bf16[512,768]{1,0:T(8,128)(2,1)S(1)} custom-call(s32[3]{0:T(128)S(1)} %pad_add_fusion.where_ref, bf16[512,768]{1,0:T(8,128)(2,1)S(1)} %all_gather.7.tok_ref), custom_call_target="tpu_custom_call" | custom-call | tf_op jit(solution)/shard_map/pallas_call | solution.py:361
  93.2 0.7 all-to-all-done.2.w_ref
  93.9 2.1 %shard_map.113 = (bf16[128,768]{1,0:T(8,128)(2,1)S(1)}, bf16[128,768]{1,0:T(8,128)(2,1)S(1)}, bf16[768,768]{1,0:T(8,128)(2,1)S(1)}, bf16[768,768]{1,0:T(8,128)(2,1)S(1)}) custom-call(s32[3]{0:T(128)S(1)} %pad_add_fusion.where_ref, bf16[512,768]{1,0:T(8,128)(2,1)S(1)} %shard_map.112.tok_ref, bf16[8,1152,128]{2,1,0:T(8,128)(2,1)S(1)} %all-to-all-done.2.w_ref), custom_call_target="tpu_custom_call" | custom-call | tf_op jit(solution)/shard_map/pallas_call | solution.py:366
  96.0 2.4 %shard_map.114 = (bf16[128,768]{1,0:T(8,128)(2,1)S(1)}, bf16[128,768]{1,0:T(8,128)(2,1)S(1)}, bf16[768,768]{1,0:T(8,128)(2,1)S(1)}) custom-call(s32[3]{0:T(128)S(1)} %pad_add_fusion.where_ref, bf16[512,768]{1,0:T(8,128)(2,1)S(1)} %shard_map.112.tok_ref, bf16[768,768]{1,0:T(8,128)(2,1)S(1)} %get-tuple-element.19.up_ref, ...), custom_call_target="tpu_custom_call" | custom-call | tf_op jit(solution)/shard_map/pallas_call | solution.py:371
  98.4 4.6 %collective-permute-start.3 = (bf16[128,768]{1,0:T(8,128)(2,1)S(1)}, bf16[128,768]{1,0:T(8,128)(2,1)S(1)}, u32[]{:S(2)}, u32[]{:S(2)}) collective-permute-start(bf16[128,768]{1,0:T(8,128)(2,1)S(1)} %get-tuple-element.22), channel_id=1, source_target_pairs={{0,1},{1,0},{2,3},{3,2},{4,5},{5,4},{6,7},{7,6},{8,9},{9,8},{10,11... | collective-permute-start | bytes 589832 | tf_op jit(solution)/shard_map/ppermute | solution.py:256
  103.0 2.2 %collective-permute-start.4 = (bf16[128,768]{1,0:T(8,128)(2,1)S(1)}, bf16[128,768]{1,0:T(8,128)(2,1)S(1)}, u32[]{:S(2)}, u32[]{:S(2)}) collective-permute-start(bf16[128,768]{1,0:T(8,128)(2,1)S(1)} %get-tuple-element.23), channel_id=1, source_target_pairs={{0,2},{1,3},{2,0},{3,1},{4,6},{5,7},{6,4},{7,5},{8,10},{9,11},{10,... | collective-permute-start | bytes 589832 | tf_op jit(solution)/shard_map/ppermute | solution.py:256
  105.2 3.2 %collective-permute-start.5 = (bf16[128,768]{1,0:T(8,128)(2,1)S(1)}, bf16[128,768]{1,0:T(8,128)(2,1)S(1)}, u32[]{:S(2)}, u32[]{:S(2)}) collective-permute-start(bf16[128,768]{1,0:T(8,128)(2,1)S(1)} %get-tuple-element.24), channel_id=1, source_target_pairs={{0,3},{1,2},{2,1},{3,0},{4,7},{5,6},{6,5},{7,4},{8,11},{9,10},{10,... | collective-permute-start | bytes 589832 | tf_op jit(solution)/shard_map/ppermute | solution.py:256
  108.5 2.9 %collective-permute-done.4.same_ref = bf16[128,768]{1,0:T(8,128)(2,1)S(1)} collective-permute-done((bf16[128,768]{1,0:T(8,128)(2,1)S(1)}, bf16[128,768]{1,0:T(8,128)(2,1)S(1)}, u32[]{:S(2)}, u32[]{:S(2)}) %collective-permute-start.4) | collective-permute-done | bytes 196640 | tf_op jit(solution)/shard_map/ppermute | solution.py:256
  111.3 4.4 %collective-permute-done.5.cross_ref = bf16[128,768]{1,0:T(8,128)(2,1)S(1)} collective-permute-done((bf16[128,768]{1,0:T(8,128)(2,1)S(1)}, bf16[128,768]{1,0:T(8,128)(2,1)S(1)}, u32[]{:S(2)}, u32[]{:S(2)}) %collective-permute-start.5) | collective-permute-done | bytes 196640 | tf_op jit(solution)/shard_map/ppermute | solution.py:256
  115.7 2.1 %shard_map.115 = bf16[128,768]{1,0:T(8,128)(2,1)} custom-call(s32[3]{0:T(128)S(1)} %pad_add_fusion.where_ref, bf16[128,768]{1,0:T(8,128)(2,1)S(1)} %get-tuple-element.21.own_ref, bf16[128,768]{1,0:T(8,128)(2,1)S(1)} %collective-permute-done.3.sibling_ref, bf16[128,768]{1,0:T(8,128)(2,1)S(1)} %collective-permute-done.4.same_ref, ...), custom_call_target="tpu_custom_call" | custom-call | tf_op jit(solution)/shard_map/pallas_call | solution.py:375
  (30 shorter events, 0.5 us)
Async XLA Ops:
  0.0 12.5 %copy-start.5 = (bf16[1,1,4,32,256]{4,3,2,1,0:T(8,128)(2,1)S(1)}, bf16[1,1,4,32,256]{4,3,2,1,0:T(8,128)(2,1)}, u32[]{:S(2)}) copy-start(bf16[1,1,4,32,256]{4,3,2,1,0:T(8,128)(2,1)} %param.11) | copy-start | bytes 196612
  2.2 23.2 %all-to-all-start = ((bf16[16,108,128]{2,1,0:T(8,128)(2,1)}), bf16[16,108,128]{2,1,0:T(8,128)(2,1)S(1)}, u32[]{:S(2)}, u32[]{:S(2)}) async-start(bf16[16,108,128]{2,1,0:T(8,128)(2,1)} %shard_map.109), calls=%async_computation | async-start | bytes 917504 | tf_op jit(solution)/shard_map/all_to_all | solution.py:264
  12.5 5.3 %collective-permute-start = (bf16[2,32,256]{2,1,0:T(8,128)(2,1)S(1)}, bf16[2,32,256]{2,1,0:T(8,128)(2,1)S(1)}, u32[]{:S(2)}, u32[]{:S(2)}) collective-permute-start(bf16[2,32,256]{2,1,0:T(8,128)(2,1)S(1)} %get-tuple-element.30), channel_id=1, source_target_pairs={{0,4},{4,8},{8,12},{12,16},{16,20},{20,24},{24,28},{28,32},{32,36}... | collective-permute-start | bytes 98312 | tf_op jit(solution)/shard_map/ppermute | solution.py:299
  16.5 7.0 %collective-permute-start.1 = (bf16[2,32,256]{2,1,0:T(8,128)(2,1)S(1)}, bf16[2,32,256]{2,1,0:T(8,128)(2,1)S(1)}, u32[]{:S(2)}, u32[]{:S(2)}) collective-permute-start(bf16[2,32,256]{2,1,0:T(8,128)(2,1)S(1)} %get-tuple-element.31), channel_id=1, source_target_pairs={{4,0},{8,4},{12,8},{16,12},{20,16},{24,20},{28,24},{32,28},{36,32}... | collective-permute-start | bytes 98312 | tf_op jit(solution)/shard_map/ppermute | solution.py:300
  27.0 29.4 %all-to-all-start.1 = ((bf16[8,576,128]{2,1,0:T(8,128)(2,1)}), bf16[8,576,128]{2,1,0:T(8,128)(2,1)S(1)}, u32[]{:S(2)}, u32[]{:S(2)}) async-start(bf16[8,576,128]{2,1,0:T(8,128)(2,1)} %broadcast_in_dim.11), calls=%async_computation.1 | async-start | bytes 2359296 | tf_op jit(solution)/shard_map/all_to_all | solution.py:264
  58.1 7.5 %copy-start.6 = (f32[768]{0:T(1024)S(1)}, f32[768]{0:T(1024)}, u32[]{:S(2)}) copy-start(f32[768]{0:T(1024)} %param.16) | copy-start | bytes 9220
  58.1 35.8 %all-to-all-start.2 = ((bf16[8,1152,128]{2,1,0:T(8,128)(2,1)}), bf16[8,1152,128]{2,1,0:T(8,128)(2,1)S(1)}, u32[]{:S(2)}, u32[]{:S(2)}) async-start(bf16[8,1152,128]{2,1,0:T(8,128)(2,1)} %broadcast_in_dim.12), calls=%async_computation.2 | async-start | bytes 4718592 | tf_op jit(solution)/shard_map/all_to_all | solution.py:264
  61.9 6.3 %collective-permute-start.2 = (bf16[8,576,128]{2,1,0:T(8,128)(2,1)S(1)}, bf16[8,576,128]{2,1,0:T(8,128)(2,1)}, u32[]{:S(2)}, u32[]{:S(2)}) collective-permute-start(bf16[8,576,128]{2,1,0:T(8,128)(2,1)S(1)} %all-to-all-done.1.own_ref), channel_id=1, source_target_pairs={{0,1},{1,0},{2,3},{3,2},{4,5},{5,4},{6,7},{7,6},{8,9},{9,8},{10,11... | collective-permute-start | bytes 3538952 | tf_op jit(solution)/shard_map/ppermute | solution.py:256
  66.3 11.3 %copy-start.1 = (bf16[1,1,4,32,768]{4,3,2,1,0:T(8,128)(2,1)S(1)}, bf16[1,1,4,32,768]{4,3,2,1,0:T(8,128)(2,1)}, u32[]{:S(2)}) copy-start(bf16[1,1,4,32,768]{4,3,2,1,0:T(8,128)(2,1)} %param.15) | copy-start | bytes 589828
  66.3 11.3 %copy-start.2 = (bf16[1,1,4,32,768]{4,3,2,1,0:T(8,128)(2,1)S(1)}, bf16[1,1,4,32,768]{4,3,2,1,0:T(8,128)(2,1)}, u32[]{:S(2)}) copy-start(bf16[1,1,4,32,768]{4,3,2,1,0:T(8,128)(2,1)} %param.14) | copy-start | bytes 589828
  66.3 11.3 %copy-start.3 = (s32[1,1,4,4]{3,2,1,0:T(4,128)S(1)}, s32[1,1,4,4]{3,2,1,0:T(4,128)}, u32[]{:S(2)}) copy-start(s32[1,1,4,4]{3,2,1,0:T(4,128)} %param.19) | copy-start | bytes 196
  66.3 11.3 %copy-start.4 = (s32[1,1,4,4]{3,2,1,0:T(4,128)S(1)}, s32[1,1,4,4]{3,2,1,0:T(4,128)}, u32[]{:S(2)}) copy-start(s32[1,1,4,4]{3,2,1,0:T(4,128)} %param.20) | copy-start | bytes 196
  96.0 19.7 %copy-start = (f32[128,768]{1,0:T(8,128)S(1)}, f32[128,768]{1,0:T(8,128)}, u32[]{:S(2)}) copy-start(f32[128,768]{1,0:T(8,128)} %get-tuple-element.26.residual_ref) | copy-start | bytes 1179652
  98.4 10.1 %collective-permute-start.3 = (bf16[128,768]{1,0:T(8,128)(2,1)S(1)}, bf16[128,768]{1,0:T(8,128)(2,1)S(1)}, u32[]{:S(2)}, u32[]{:S(2)}) collective-permute-start(bf16[128,768]{1,0:T(8,128)(2,1)S(1)} %get-tuple-element.22), channel_id=1, source_target_pairs={{0,1},{1,0},{2,3},{3,2},{4,5},{5,4},{6,7},{7,6},{8,9},{9,8},{10,11... | collective-permute-start | bytes 589832 | tf_op jit(solution)/shard_map/ppermute | solution.py:256
  103.0 8.3 %collective-permute-start.4 = (bf16[128,768]{1,0:T(8,128)(2,1)S(1)}, bf16[128,768]{1,0:T(8,128)(2,1)S(1)}, u32[]{:S(2)}, u32[]{:S(2)}) collective-permute-start(bf16[128,768]{1,0:T(8,128)(2,1)S(1)} %get-tuple-element.23), channel_id=1, source_target_pairs={{0,2},{1,3},{2,0},{3,1},{4,6},{5,7},{6,4},{7,5},{8,10},{9,11},{10,... | collective-permute-start | bytes 589832 | tf_op jit(solution)/shard_map/ppermute | solution.py:256
  105.2 10.5 %collective-permute-start.5 = (bf16[128,768]{1,0:T(8,128)(2,1)S(1)}, bf16[128,768]{1,0:T(8,128)(2,1)S(1)}, u32[]{:S(2)}, u32[]{:S(2)}) collective-permute-start(bf16[128,768]{1,0:T(8,128)(2,1)S(1)} %get-tuple-element.24), channel_id=1, source_target_pairs={{0,3},{1,2},{2,1},{3,0},{4,7},{5,6},{6,5},{7,4},{8,11},{9,10},{10,... | collective-permute-start | bytes 589832 | tf_op jit(solution)/shard_map/ppermute | solution.py:256

commit v2 on v1

--- a/solution.py
+++ b/solution.py
@@ -146,26 +146,32 @@
     return 0.5 * v * (1.0 + jnp.tanh(0.7978845608028654 * (v + 0.044715 * (v * v * v))))
 
 
-def two_blocks(where_ref, tok_ref, up_ref, down_ref, out_refs, chip_flip):
-    view = where_ref[2]
-    for out_ref, flip in zip(out_refs, (0, 1)):
-        rows = pl.ds(pl.multiple_of((view ^ (chip_flip * 2 + flip)) * 128, 128), 128)
-        hidden = gelu(jnp.dot(tok_ref[rows, :], up_ref[...], preferred_element_type=F32)).astype(BF)
-        out_ref[...] = last_dims(hidden, down_ref[...]).astype(BF)
-
-
-def far_kernel(where_ref, tok_ref, w_ref, same_ref, cross_ref, up_ref, down_ref):
-    for tile in range(6):
-        cols = slice(tile * 128, (tile + 1) * 128)
-        for d in range(8):
-            rows = slice(d * 96, (d + 1) * 96)
-            up_ref[rows, cols] = w_ref[d, tile * 96 : (tile + 1) * 96, :]
-            down_ref[rows, cols] = w_ref[d, 576 + tile * 96 : 576 + (tile + 1) * 96, :]
-    two_blocks(where_ref, tok_ref, up_ref, down_ref, (same_ref, cross_ref), 1)
-
-
-def near_kernel(where_ref, tok_ref, up_ref, down_ref, own_ref, sibling_ref, swap_ref):
-    two_blocks(where_ref, tok_ref, up_ref, down_ref, (own_ref, sibling_ref), 0)
+def two_blocks(where_ref, tok_ref, w_ref, out_refs, chip_flip):
+    blocks = []
+    for flip in range(2):
+        view = where_ref[2] ^ (chip_flip * 2 + flip)
+        blocks.append(tok_ref[pl.ds(pl.multiple_of(view * 128, 128), 128), :])
+
+    def gathered(at):
+        tiles = []
+        for tile in range(6):
+            rows = slice(at + tile * 96, at + (tile + 1) * 96)
+            tiles.append(jnp.concatenate([w_ref[d, rows, :] for d in range(8)], axis=0))
+        return jnp.concatenate(tiles, axis=1)
+
+    tokens = jnp.concatenate(blocks, axis=0)
+    hidden = gelu(jnp.dot(tokens, gathered(0), preferred_element_type=F32)).astype(BF)
+    parts = last_dims(hidden, gathered(576)).astype(BF)
+    for k, out_ref in enumerate(out_refs):
+        out_ref[...] = parts[k * 128 : (k + 1) * 128]
+
+
+def far_kernel(where_ref, tok_ref, w_ref, same_ref, cross_ref):
+    two_blocks(where_ref, tok_ref, w_ref, (same_ref, cross_ref), 1)
+
+
+def near_kernel(where_ref, tok_ref, w_ref, own_ref, sibling_ref, swap_ref):
+    two_blocks(where_ref, tok_ref, w_ref, (own_ref, sibling_ref), 0)
     swap_ref[...] = one_hot(768, 6)
 
 
@@ -189,7 +195,8 @@
     even = jnp.where(first, alike, unlike)
     high = odd.astype(BF)
     low = (odd - high.astype(F32)).astype(BF)
-    odd = last_dims(high, swap_ref[...]) + last_dims(low, swap_ref[...])
+    both = last_dims(jnp.concatenate([high, low], axis=0), swap_ref[...])
+    odd = both[:128] + both[128:]
     out_ref[...] = (residual_ref[...] + (even + odd)).astype(BF)
 
 
@@ -294,12 +301,6 @@
     core = view_id % 2
     first_row = lax.axis_index(SLAB) * 4
     where = jnp.stack([core, first_row, view_id]).astype(jnp.int32)
-    feats = latent_feats[0, 0]
-    ends = lax.axis_size(SLAB) - 1
-    above = lax.ppermute(feats[2:], SLAB, [(i, i + 1) for i in range(ends)])
-    below = lax.ppermute(feats[:2], SLAB, [(i + 1, i) for i in range(ends)])
-    rows = jnp.concatenate([above, feats, below], axis=0).reshape(256, 256)
-
     even = core == 0
     mine = kernel_call(
         pack_kernel,
@@ -311,7 +312,11 @@
     wide = by_core((1, 2), (0, 1))
     long = by_core((0,), (2,))
     near = exchange(mine, wide)
-    near, rows = lax.optimization_barrier((near, rows))
+    near, feats = lax.optimization_barrier((near, latent_feats[0, 0]))
+    ends = lax.axis_size(SLAB) - 1
+    above = lax.ppermute(feats[2:], SLAB, [(i, i + 1) for i in range(ends)])
+    below = lax.ppermute(feats[:2], SLAB, [(i + 1, i) for i in range(ends)])
+    rows = jnp.concatenate([above, feats, below], axis=0).reshape(256, 256)
     code = jnp.where(
         even, regroup(near[:, :36], 18), jnp.pad(regroup(near[:, :24], 2), ((0, 192), (0, 0)))
     )
@@ -363,14 +368,12 @@
     )(where, tokens)
     block = jax.ShapeDtypeStruct((128, 768), BF)
     square = jax.ShapeDtypeStruct((768, 768), BF)
-    same, cross, up, down = kernel_call(
-        far_kernel, (block, block, square, square), [SMEM, VMEM, VMEM]
-    )(where, tokens, mlp)
+    same, cross = kernel_call(far_kernel, (block, block), [SMEM, VMEM, VMEM])(where, tokens, mlp)
     cross = to_view(cross, 3)
     same = to_view(same, 2)
     own, sibling, swap = kernel_call(
-        near_kernel, (block, block, square), [SMEM] + [VMEM] * 3
-    )(where, tokens, up, down)
+        near_kernel, (block, block, square), [SMEM, VMEM, VMEM]
+    )(where, tokens, mlp)
     sibling = to_view(sibling, 1)
     result = kernel_call(
         sum_kernel, block, [SMEM] + [VMEM] * 6

time: 119 us -> 133 us (1.12)
  waiting for transfers between devices: 35.9 us -> 54.7 us
  starting transfers between devices: 42.9 us -> 39.3 us
  Pallas kernels: 18.5 us -> 17.1 us
    ppermute x1, waiting for transfers between devices: 0.01 us -> 16.4 us  [shards(): above = lax.ppermute(feats[2:], SLAB, [(i, i + 1) for i in range(ends)])]
    all_to_all x3, waiting for transfers between devices: 21.2 us -> 32.2 us  [exchange(): lax.all_to_all(copies, ('dp', 'slab_0', 'slab_1', 'view'), split_axis=0,...]
    ppermute x4, waiting for transfers between devices: 9.09 us -> 2.96 us  [to_view(): return lax.ppermute(value, 'view', [(i, i ^ flip) for i in range(4)])]
    ppermute x4, starting transfers between devices: 13.7 us -> 11.1 us  [to_view(): return lax.ppermute(value, 'view', [(i, i ^ flip) for i in range(4)])]
    ppermute x1, waiting for transfers between devices: 5.64 us -> 3.1 us  [shards(): below = lax.ppermute(feats[:2], SLAB, [(i + 1, i) for i in range(ends)])]
  transfers between devices with their start and end apart: 9 -> 9, of which waited for: 7 -> 5; matrix products, arithmetic and copies ran while one was open for 1% -> 2% of each run, Pallas kernels for 8% -> 9%
where the time goes in v2:
time: 133 us; the launch traced here: 132 us
  waiting for transfers between devices  54.7 us (41%)
  starting transfers between devices  39.3 us (30%)
  Pallas kernels  17.1 us (13%)
  blocking collectives  14.3 us (11%)
  local copies, waits for them, and re-layouts  4.28 us (3%)
  other arithmetic  2.34 us (2%)
    all_to_all x3, waiting for transfers between devices, exchange(): lax.all_to_all(copies, ('dp', 'slab_0', 'slab_1', 'view'), split_axis=0,...  32.2 us
    all_to_all x3, starting transfers between devices, exchange(): lax.all_to_all(copies, ('dp', 'slab_0', 'slab_1', 'view'), split_axis=0,...  23.8 us
    ppermute x1, waiting for transfers between devices, shards(): above = lax.ppermute(feats[2:], SLAB, [(i, i + 1) for i in range(ends)])  16.4 us
    ppermute x4, starting transfers between devices, to_view(): return lax.ppermute(value, 'view', [(i, i ^ flip) for i in range(4)])  11.1 us
    all_gather x1, blocking collectives, shards(): tokens = lax.all_gather(normed, 'view', axis=0, tiled=True)  8.71 us
    all_gather x1, blocking collectives, shards(): nearby = lax.all_gather(encoded, 'view', axis=0, tiled=True)  5.6 us
    pallas_call x1, Pallas kernels, shards(): kernel_call(attention_kernel, (jax.ShapeDtypeStruct((128, 768), BF), pltp...  5.44 us
    ppermute x1, waiting for transfers between devices, shards(): below = lax.ppermute(feats[:2], SLAB, [(i + 1, i) for i in range(ends)])  3.1 us
  transfers between devices with their start and end apart: 9, of which 5 were waited for; matrix products, arithmetic and copies ran while one was open for 2% of the time, Pallas kernels for 9%

profile of v2, /device:TPU:1, one launch (start us, length us, event | category | flops | bytes accessed | tf_op | source)
XLA Modules:
  0.0 132.3 jit_solution(15722449776767648104)
XLA Ops:
  0.0 0.1 pad_add_fusion.where_ref
  0.1 2.2 %shard_map.109 = bf16[16,108,128]{2,1,0:T(8,128)(2,1)} custom-call(s32[3]{0:T(128)S(1)} %pad_add_fusion.where_ref, bf16[18,256]{1,0:T(8,128)(2,1)} %refs_0_.1, bf16[2,1536]{1,0:T(2,128)(2,1)} %refs_1_.1, bf16[6,768]{1,0:T(8,128)(2,1)} %refs_2_.1, bf16[6,768]{1,0:T(8,128)(2,1)} %refs_3_.1), custom_call_target="tpu_custom_call" | custom-call | tf_op jit(solution)/shard_map/pallas_call | solution.py:305
  2.2 10.2 %all-to-all-start = ((bf16[16,108,128]{2,1,0:T(8,128)(2,1)}), bf16[16,108,128]{2,1,0:T(8,128)(2,1)S(1)}, u32[]{:S(2)}, u32[]{:S(2)}) async-start(bf16[16,108,128]{2,1,0:T(8,128)(2,1)} %shard_map.109), calls=%async_computation | async-start | bytes 917504 | tf_op jit(solution)/shard_map/all_to_all | solution.py:271
  12.5 13.0 %all-to-all-done = bf16[16,108,128]{2,1,0:T(8,128)(2,1)S(1)} async-done(((bf16[16,108,128]{2,1,0:T(8,128)(2,1)}), bf16[16,108,128]{2,1,0:T(8,128)(2,1)S(1)}, u32[]{:S(2)}, u32[]{:S(2)}) %all-to-all-start) | async-done | bytes 442400 | tf_op jit(solution)/shard_map/all_to_all | solution.py:271
  25.5 0.1 fusion
  25.6 0.1 copy.18
  25.9 1.2 broadcast_in_dim.11
  27.1 9.8 %all-to-all-start.1 = ((bf16[8,576,128]{2,1,0:T(8,128)(2,1)}), bf16[8,576,128]{2,1,0:T(8,128)(2,1)S(1)}, u32[]{:S(2)}, u32[]{:S(2)}) async-start(bf16[8,576,128]{2,1,0:T(8,128)(2,1)} %broadcast_in_dim.11), calls=%async_computation.1 | async-start | bytes 2359296 | tf_op jit(solution)/shard_map/all_to_all | solution.py:271
  37.1 0.1 reshape.44
  37.2 19.2 %all-to-all-done.1.own_ref = bf16[8,576,128]{2,1,0:T(8,128)(2,1)S(1)} async-done(((bf16[8,576,128]{2,1,0:T(8,128)(2,1)}), bf16[8,576,128]{2,1,0:T(8,128)(2,1)S(1)}, u32[]{:S(2)}, u32[]{:S(2)}) %all-to-all-start.1) | async-done | bytes 1179680 | tf_op jit(solution)/shard_map/all_to_all | solution.py:271
  56.4 1.8 %broadcast_in_dim.12 = bf16[8,1152,128]{2,1,0:T(8,128)(2,1)} broadcast(bf16[1152,128]{1,0:T(8,128)(2,1)S(1)} %pad_maximum_fusion), dimensions={1,2} | broadcast | bytes 2654208 | tf_op jit(solution)/shard_map/broadcast_in_dim | solution.py:267
  58.1 3.7 %all-to-all-start.2 = ((bf16[8,1152,128]{2,1,0:T(8,128)(2,1)}), bf16[8,1152,128]{2,1,0:T(8,128)(2,1)S(1)}, u32[]{:S(2)}, u32[]{:S(2)}) async-start(bf16[8,1152,128]{2,1,0:T(8,128)(2,1)} %broadcast_in_dim.12), calls=%async_computation.2 | async-start | bytes 4718592 | tf_op jit(solution)/shard_map/all_to_all | solution.py:271
  61.9 3.4 %collective-permute-start.2 = (bf16[8,576,128]{2,1,0:T(8,128)(2,1)S(1)}, bf16[8,576,128]{2,1,0:T(8,128)(2,1)}, u32[]{:S(2)}, u32[]{:S(2)}) collective-permute-start(bf16[8,576,128]{2,1,0:T(8,128)(2,1)S(1)} %all-to-all-done.1.own_ref), channel_id=1, source_target_pairs={{0,1},{1,0},{2,3},{3,2},{4,5},{5,4},{6,7},{7,6},{8,9},{9,8},{10,11... | collective-permute-start | bytes 3538952 | tf_op jit(solution)/shard_map/ppermute | solution.py:263
  65.3 0.8 fusion.1
  66.1 3.1 %collective-permute-start = (bf16[2,32,256]{2,1,0:T(8,128)(2,1)S(1)}, bf16[2,32,256]{2,1,0:T(8,128)(2,1)S(1)}, u32[]{:S(2)}, u32[]{:S(2)}) collective-permute-start(bf16[2,32,256]{2,1,0:T(8,128)(2,1)S(1)} %get-tuple-element.26), channel_id=1, source_target_pairs={{0,4},{4,8},{8,12},{12,16},{16,20},{20,24},{24,28},{28,32},{32,36}... | collective-permute-start | bytes 98312 | tf_op jit(solution)/shard_map/ppermute | solution.py:317
  69.2 1.3 collective-permute-start.1
  70.5 0.7 compare_select_fusion.seen_ref
  71.2 16.4 %collective-permute-done = bf16[2,32,256]{2,1,0:T(8,128)(2,1)S(1)} collective-permute-done((bf16[2,32,256]{2,1,0:T(8,128)(2,1)S(1)}, bf16[2,32,256]{2,1,0:T(8,128)(2,1)S(1)}, u32[]{:S(2)}, u32[]{:S(2)}) %collective-permute-start) | collective-permute-done | bytes 32800 | tf_op jit(solution)/shard_map/ppermute | solution.py:317
  87.6 3.1 %collective-permute-done.1 = bf16[2,32,256]{2,1,0:T(8,128)(2,1)S(1)} collective-permute-done((bf16[2,32,256]{2,1,0:T(8,128)(2,1)S(1)}, bf16[2,32,256]{2,1,0:T(8,128)(2,1)S(1)}, u32[]{:S(2)}, u32[]{:S(2)}) %collective-permute-start.1) | collective-permute-done | bytes 32800 | tf_op jit(solution)/shard_map/ppermute | solution.py:318
  90.7 1.5 %pad_maximum_fusion.1 = bf16[8,32,256]{2,1,0:T(8,128)(2,1)} fusion(bf16[2,32,256]{2,1,0:T(8,128)(2,1)S(1)} %collective-permute-done.1, bf16[4,32,256]{2,1,0:T(8,128)(2,1)} %bitcast.36, bf16[2,32,256]{2,1,0:T(8,128)(2,1)S(1)} %collective-permute-done), kind=kLoop, calls=%fused_computation.2 | loop fusion | flops 131072 | bytes 262144 | tf_op jit(solution)/shard_map/concatenate | solution.py:319
  92.2 2.9 %shard_map.110 = bf16[192,256]{1,0:T(8,128)(2,1)S(1)} custom-call(s32[3]{0:T(128)S(1)} %pad_add_fusion.where_ref, bf16[256,256]{1,0:T(8,128)(2,1)} %bitcast.32, bf16[8,576,128]{2,1,0:T(8,128)(2,1)S(1)} %all-to-all-done.1.own_ref, bf16[8,576,128]{2,1,0:T(8,128)(2,1)} %collective-permute-done.2.other_ref), custom_call_target="tpu_custom_call" | custom-call | tf_op jit(solution)/shard_map/pallas_call | solution.py:330
  95.1 5.6 %all_gather.6.enc_ref = bf16[768,256]{1,0:T(8,128)(2,1)S(1)} all-gather(bf16[192,256]{1,0:T(8,128)(2,1)S(1)} %shard_map.110), channel_id=1, replica_groups=mesh['dp'=8,'slab_0'=2,'slab_1'=8,'view'=4] {'view'}, dimensions={0}, use_global_device_ids=true | all-gather | bytes 491520 | tf_op jit(solution)/shard_map/all_gather | solution.py:339
  100.8 5.4 %shard_map.111 = (bf16[128,768]{1,0:T(8,128)(2,1)S(1)}, f32[128,768]{1,0:T(8,128)}) custom-call(s32[3]{0:T(128)S(1)} %pad_add_fusion.where_ref, s32[4,4]{1,0:T(4,128)S(1)} %bitcast.27, s32[4,4]{1,0:T(4,128)S(1)} %bitcast.28, s32[4]{0:T(128)S(1)} %compare_select_fusion.seen_ref, bf16[768,256]{1,0:T(8,128)(2,1)S(1)} %all_gather.6.enc_ref, ...), custom_call_target="tpu_custom_call" | custom-call | tf_op jit(solution)/shard_map/pallas_call | solution.py:342
  106.2 8.7 %all_gather.7.tok_ref = bf16[512,768]{1,0:T(8,128)(2,1)S(1)} all-gather(bf16[128,768]{1,0:T(8,128)(2,1)S(1)} %get-tuple-element.16), channel_id=1, replica_groups=mesh['dp'=8,'slab_0'=2,'slab_1'=8,'view'=4] {'view'}, dimensions={0}, use_global_device_ids=true | all-gather | bytes 983040 | tf_op jit(solution)/shard_map/all_gather | solution.py:365
  114.9 1.4 %shard_map.112.tok_ref = bf16[512,768]{1,0:T(8,128)(2,1)S(1)} custom-call(s32[3]{0:T(128)S(1)} %pad_add_fusion.where_ref, bf16[512,768]{1,0:T(8,128)(2,1)S(1)} %all_gather.7.tok_ref), custom_call_target="tpu_custom_call" | custom-call | tf_op jit(solution)/shard_map/pallas_call | solution.py:366
  116.3 1.5 %shard_map.114 = (bf16[128,768]{1,0:T(8,128)(2,1)S(1)}, bf16[128,768]{1,0:T(8,128)(2,1)S(1)}) custom-call(s32[3]{0:T(128)S(1)} %pad_add_fusion.where_ref, bf16[512,768]{1,0:T(8,128)(2,1)S(1)} %shard_map.112.tok_ref, bf16[8,1152,128]{2,1,0:T(8,128)(2,1)S(1)} %all-to-all-done.2.w_ref), custom_call_target="tpu_custom_call" | custom-call | tf_op jit(solution)/shard_map/pallas_call | solution.py:371
  117.8 3.2 %collective-permute-start.4 = (bf16[128,768]{1,0:T(8,128)(2,1)S(1)}, bf16[128,768]{1,0:T(8,128)(2,1)S(1)}, u32[]{:S(2)}, u32[]{:S(2)}) collective-permute-start(bf16[128,768]{1,0:T(8,128)(2,1)S(1)} %get-tuple-element.19), channel_id=1, source_target_pairs={{0,2},{1,3},{2,0},{3,1},{4,6},{5,7},{6,4},{7,5},{8,10},{9,11},{10,... | collective-permute-start | bytes 589832 | tf_op jit(solution)/shard_map/ppermute | solution.py:263
  121.0 2.1 %collective-permute-start.5 = (bf16[128,768]{1,0:T(8,128)(2,1)S(1)}, bf16[128,768]{1,0:T(8,128)(2,1)S(1)}, u32[]{:S(2)}, u32[]{:S(2)}) collective-permute-start(bf16[128,768]{1,0:T(8,128)(2,1)S(1)} %get-tuple-element.20), channel_id=1, source_target_pairs={{0,3},{1,2},{2,1},{3,0},{4,7},{5,6},{6,5},{7,4},{8,11},{9,10},{10,... | collective-permute-start | bytes 589832 | tf_op jit(solution)/shard_map/ppermute | solution.py:263
  123.1 2.0 %shard_map.113 = (bf16[128,768]{1,0:T(8,128)(2,1)S(1)}, bf16[128,768]{1,0:T(8,128)(2,1)S(1)}, bf16[768,768]{1,0:T(8,128)(2,1)S(1)}) custom-call(s32[3]{0:T(128)S(1)} %pad_add_fusion.where_ref, bf16[512,768]{1,0:T(8,128)(2,1)S(1)} %shard_map.112.tok_ref, bf16[8,1152,128]{2,1,0:T(8,128)(2,1)S(1)} %all-to-all-done.2.w_ref), custom_call_target="tpu_custom_call" | custom-call | tf_op jit(solution)/shard_map/pallas_call | solution.py:374
  125.1 2.5 %collective-permute-start.3 = (bf16[128,768]{1,0:T(8,128)(2,1)S(1)}, bf16[128,768]{1,0:T(8,128)(2,1)S(1)}, u32[]{:S(2)}, u32[]{:S(2)}) collective-permute-start(bf16[128,768]{1,0:T(8,128)(2,1)S(1)} %get-tuple-element.18), channel_id=1, source_target_pairs={{0,1},{1,0},{2,3},{3,2},{4,5},{5,4},{6,7},{7,6},{8,9},{9,8},{10,11... | collective-permute-start | bytes 589832 | tf_op jit(solution)/shard_map/ppermute | solution.py:263
  127.6 3.0 %collective-permute-done.5.cross_ref = bf16[128,768]{1,0:T(8,128)(2,1)S(1)} collective-permute-done((bf16[128,768]{1,0:T(8,128)(2,1)S(1)}, bf16[128,768]{1,0:T(8,128)(2,1)S(1)}, u32[]{:S(2)}, u32[]{:S(2)}) %collective-permute-start.5) | collective-permute-done | bytes 196640 | tf_op jit(solution)/shard_map/ppermute | solution.py:263
  130.5 1.8 %shard_map.115 = bf16[128,768]{1,0:T(8,128)(2,1)} custom-call(s32[3]{0:T(128)S(1)} %pad_add_fusion.where_ref, bf16[128,768]{1,0:T(8,128)(2,1)S(1)} %get-tuple-element.17.own_ref, bf16[128,768]{1,0:T(8,128)(2,1)S(1)} %collective-permute-done.3.sibling_ref, bf16[128,768]{1,0:T(8,128)(2,1)S(1)} %collective-permute-done.4.same_ref, ...), custom_call_target="tpu_custom_call" | custom-call | tf_op jit(solution)/shard_map/pallas_call | solution.py:378
  (28 shorter events, 0.4 us)
Async XLA Ops:
  2.2 23.3 %all-to-all-start = ((bf16[16,108,128]{2,1,0:T(8,128)(2,1)}), bf16[16,108,128]{2,1,0:T(8,128)(2,1)S(1)}, u32[]{:S(2)}, u32[]{:S(2)}) async-start(bf16[16,108,128]{2,1,0:T(8,128)(2,1)} %shard_map.109), calls=%async_computation | async-start | bytes 917504 | tf_op jit(solution)/shard_map/all_to_all | solution.py:271
  27.1 29.3 %all-to-all-start.1 = ((bf16[8,576,128]{2,1,0:T(8,128)(2,1)}), bf16[8,576,128]{2,1,0:T(8,128)(2,1)S(1)}, u32[]{:S(2)}, u32[]{:S(2)}) async-start(bf16[8,576,128]{2,1,0:T(8,128)(2,1)} %broadcast_in_dim.11), calls=%async_computation.1 | async-start | bytes 2359296 | tf_op jit(solution)/shard_map/all_to_all | solution.py:271
  58.1 13.1 %copy-start.5 = (f32[768]{0:T(1024)S(1)}, f32[768]{0:T(1024)}, u32[]{:S(2)}) copy-start(f32[768]{0:T(1024)} %param.16) | copy-start | bytes 9220
  58.1 58.2 %all-to-all-start.2 = ((bf16[8,1152,128]{2,1,0:T(8,128)(2,1)}), bf16[8,1152,128]{2,1,0:T(8,128)(2,1)S(1)}, u32[]{:S(2)}, u32[]{:S(2)}) async-start(bf16[8,1152,128]{2,1,0:T(8,128)(2,1)} %broadcast_in_dim.12), calls=%async_computation.2 | async-start | bytes 4718592 | tf_op jit(solution)/shard_map/all_to_all | solution.py:271
  61.9 30.3 %collective-permute-start.2 = (bf16[8,576,128]{2,1,0:T(8,128)(2,1)S(1)}, bf16[8,576,128]{2,1,0:T(8,128)(2,1)}, u32[]{:S(2)}, u32[]{:S(2)}) collective-permute-start(bf16[8,576,128]{2,1,0:T(8,128)(2,1)S(1)} %all-to-all-done.1.own_ref), channel_id=1, source_target_pairs={{0,1},{1,0},{2,3},{3,2},{4,5},{5,4},{6,7},{7,6},{8,9},{9,8},{10,11... | collective-permute-start | bytes 3538952 | tf_op jit(solution)/shard_map/ppermute | solution.py:263
  66.1 21.5 %collective-permute-start = (bf16[2,32,256]{2,1,0:T(8,128)(2,1)S(1)}, bf16[2,32,256]{2,1,0:T(8,128)(2,1)S(1)}, u32[]{:S(2)}, u32[]{:S(2)}) collective-permute-start(bf16[2,32,256]{2,1,0:T(8,128)(2,1)S(1)} %get-tuple-element.26), channel_id=1, source_target_pairs={{0,4},{4,8},{8,12},{12,16},{16,20},{20,24},{24,28},{28,32},{32,36}... | collective-permute-start | bytes 98312 | tf_op jit(solution)/shard_map/ppermute | solution.py:317
  69.2 21.5 %collective-permute-start.1 = (bf16[2,32,256]{2,1,0:T(8,128)(2,1)S(1)}, bf16[2,32,256]{2,1,0:T(8,128)(2,1)S(1)}, u32[]{:S(2)}, u32[]{:S(2)}) collective-permute-start(bf16[2,32,256]{2,1,0:T(8,128)(2,1)S(1)} %get-tuple-element.27), channel_id=1, source_target_pairs={{4,0},{8,4},{12,8},{16,12},{20,16},{24,20},{28,24},{32,28},{36,32}... | collective-permute-start | bytes 98312 | tf_op jit(solution)/shard_map/ppermute | solution.py:318
  92.2 8.6 %copy-start.1 = (bf16[1,1,4,32,768]{4,3,2,1,0:T(8,128)(2,1)S(1)}, bf16[1,1,4,32,768]{4,3,2,1,0:T(8,128)(2,1)}, u32[]{:S(2)}) copy-start(bf16[1,1,4,32,768]{4,3,2,1,0:T(8,128)(2,1)} %param.15) | copy-start | bytes 589828
  92.2 8.6 %copy-start.2 = (bf16[1,1,4,32,768]{4,3,2,1,0:T(8,128)(2,1)S(1)}, bf16[1,1,4,32,768]{4,3,2,1,0:T(8,128)(2,1)}, u32[]{:S(2)}) copy-start(bf16[1,1,4,32,768]{4,3,2,1,0:T(8,128)(2,1)} %param.14) | copy-start | bytes 589828
  92.2 8.6 %copy-start.3 = (s32[1,1,4,4]{3,2,1,0:T(4,128)S(1)}, s32[1,1,4,4]{3,2,1,0:T(4,128)}, u32[]{:S(2)}) copy-start(s32[1,1,4,4]{3,2,1,0:T(4,128)} %param.19) | copy-start | bytes 196
  92.2 8.6 %copy-start.4 = (s32[1,1,4,4]{3,2,1,0:T(4,128)S(1)}, s32[1,1,4,4]{3,2,1,0:T(4,128)}, u32[]{:S(2)}) copy-start(s32[1,1,4,4]{3,2,1,0:T(4,128)} %param.20) | copy-start | bytes 196
  117.8 9.8 %collective-permute-start.4 = (bf16[128,768]{1,0:T(8,128)(2,1)S(1)}, bf16[128,768]{1,0:T(8,128)(2,1)S(1)}, u32[]{:S(2)}, u32[]{:S(2)}) collective-permute-start(bf16[128,768]{1,0:T(8,128)(2,1)S(1)} %get-tuple-element.19), channel_id=1, source_target_pairs={{0,2},{1,3},{2,0},{3,1},{4,6},{5,7},{6,4},{7,5},{8,10},{9,11},{10,... | collective-permute-start | bytes 589832 | tf_op jit(solution)/shard_map/ppermute | solution.py:263
  121.0 9.5 %copy-start = (f32[128,768]{1,0:T(8,128)S(1)}, f32[128,768]{1,0:T(8,128)}, u32[]{:S(2)}) copy-start(f32[128,768]{1,0:T(8,128)} %get-tuple-element.22.residual_ref) | copy-start | bytes 1179652
  121.0 9.5 %collective-permute-start.5 = (bf16[128,768]{1,0:T(8,128)(2,1)S(1)}, bf16[128,768]{1,0:T(8,128)(2,1)S(1)}, u32[]{:S(2)}, u32[]{:S(2)}) collective-permute-start(bf16[128,768]{1,0:T(8,128)(2,1)S(1)} %get-tuple-element.20), channel_id=1, source_target_pairs={{0,3},{1,2},{2,1},{3,0},{4,7},{5,6},{6,5},{7,4},{8,11},{9,10},{10,... | collective-permute-start | bytes 589832 | tf_op jit(solution)/shard_map/ppermute | solution.py:263
  125.1 5.5 %collective-permute-start.3 = (bf16[128,768]{1,0:T(8,128)(2,1)S(1)}, bf16[128,768]{1,0:T(8,128)(2,1)S(1)}, u32[]{:S(2)}, u32[]{:S(2)}) collective-permute-start(bf16[128,768]{1,0:T(8,128)(2,1)S(1)} %get-tuple-element.18), channel_id=1, source_target_pairs={{0,1},{1,0},{2,3},{3,2},{4,5},{5,4},{6,7},{7,6},{8,9},{9,8},{10,11... | collective-permute-start | bytes 589832 | tf_op jit(solution)/shard_map/ppermute | solution.py:263
